TPU v7x, 32 devices: a whole 2x2x4 slice. The times are simulated.
32 devices in a mesh: groups: 2 (over x), facet: 16 (over z, y, core).
Axes of the slice: x: 2, y: 2, z: 4, core: 2. Of those that a mesh axis runs over, the one named last changes fastest.
Arguments:
- sky_strips: bfloat16 [2, 16, 16384], P(None, 'groups', 'facet'), parts along dimension 1, may hold values from -6 to 6
- prolate: float32 [1024], replicated, may hold values from 0.25 to 1
- subgrid_offset: int32 [16], replicated, may hold values from 0 to 16383
- owner: int32 [16], replicated, may hold values from 0 to 15, as said below
- observed: float32 [64, 2, 8, 8192], P(('groups', 'facet')), parts along dimension 0, may hold values from -6 to 6
- vis_uv: float32 [64, 8192], P(('groups', 'facet')), parts along dimension 0, may hold values from 0 to 512
- vis_count: int32 [64], P(('groups', 'facet')), parts along dimension 0, may hold values from 1 to 8192
Outputs:
- residual_vis: bfloat16 [64, 2, 8, 8192], P(('groups', 'facet')), parts along dimension 0
- image_update: float32 [2, 16, 16384], P(None, 'groups', 'facet'), parts along dimension 1
There are 2 independent parts, one for each index of `groups`. A program takes and returns all parts, laid end to end along the dimension named above; an argument that names none is the same for every part. Nothing has to cross between parts.
Inputs may be any that keep to these rules, and one draw needn't show every extreme that they name: `owner`: each index of facet owns at most 2 subgrids, and some index owns exactly 2.
All inputs are finite; a program needn't handle non-finite values.
Results may differ from a plain program's by a relative error of at most 0.01.
Values may be sent and summed in bfloat16 or wider, within the bound.
No kernel may reach another device: no remote copies, remote signals or barrier semaphores. Data moves between devices by JAX's collectives and lax.ppermute only.
A program may use at most 64 MiB of HBM per device.

v0:
```python
import math

import jax
import jax.numpy as jnp
from jax import lax
from jax.sharding import PartitionSpec as P

POINTS = 512


TWO_PI = 6.283185307179586


def local_product(first, second):
    return jnp.dot(first, second, preferred_element_type=jnp.float32)


def modular_product(factor, second, modulus):
    upper = second // 256
    lower = second % 256
    return (factor * lower % modulus + factor * upper % modulus * 256 % modulus) % modulus


def phasor(index, modulus):
    angle = index.astype(jnp.float32) * (TWO_PI / modulus)
    return (jnp.cos(angle), jnp.sin(angle))


def forward_table(columns, points, modulus):
    across = jnp.arange(columns, dtype=jnp.int32)[:, None]
    along = jnp.arange(points, dtype=jnp.int32)[None, :]
    cosine, sine = phasor(modular_product(across, along, modulus), modulus)
    upper_half = jnp.concatenate([cosine, -sine], 1)
    lower_half = jnp.concatenate([sine, cosine], 1)
    return jnp.concatenate([upper_half, lower_half], 0).astype(jnp.bfloat16)


def facet_terms(
    strip_re, strip_im, weight, columns, anchor, offsets, phase_table, modulus, points, product
):
    scaled_re = strip_re * weight
    scaled_im = strip_im * weight
    cosine, sine = phasor(modular_product(columns[None, :], offsets[:, None], modulus), modulus)
    mod_re = scaled_re[None] * cosine[:, None] + scaled_im[None] * sine[:, None]
    mod_im = scaled_im[None] * cosine[:, None] - scaled_re[None] * sine[:, None]
    subgrid_count = offsets.shape[0]
    strip_rows = strip_re.shape[0]
    modulated = (
        jnp.concatenate([mod_re, mod_im], -1)
        .astype(jnp.bfloat16)
        .reshape(subgrid_count * strip_rows, -1)
    )
    raw = product(modulated, phase_table).reshape(subgrid_count, strip_rows, 2 * points)
    along = jnp.arange(points, dtype=jnp.int32)
    shifted = (along[None, :] + offsets[:, None]) % modulus
    out_cos, out_sin = phasor(modular_product(anchor, shifted, modulus), modulus)
    raw_re = raw[..., :points]
    raw_im = raw[..., points:]
    factor_scale = 1.0 / math.sqrt(modulus)
    term_re = (raw_re * out_cos[:, None] + raw_im * out_sin[:, None]) * factor_scale
    term_im = (raw_im * out_cos[:, None] - raw_re * out_sin[:, None]) * factor_scale
    return jnp.concatenate([term_re, term_im], -1)


def slot_layout(owner, slots, total):
    subgrid_count = owner.shape[0]
    index = jnp.arange(subgrid_count, dtype=jnp.int32)
    same = owner[:, None] == owner[None, :]
    before = index[None, :] < index[:, None]
    ranked = jnp.sum(same & before, axis=1)
    slot_of = owner * slots + ranked
    wanted = jnp.arange(total, dtype=jnp.int32)
    matches = slot_of[None, :] == wanted[:, None]
    is_held = jnp.any(matches, axis=1)
    slot_ids = jnp.sum(jnp.where(matches, index[None, :], 0), axis=1)
    return (slot_ids, is_held)


def degrid_slot(grid, observed_slot, coords, live_count, is_held, block, points, product):
    strip_rows = grid.shape[0]
    total = coords.shape[0]
    blocks = total // block
    obs_blocks = observed_slot.reshape(2, strip_rows, blocks, block).transpose(2, 0, 1, 3)
    coord_blocks = coords.reshape(blocks, block)
    along = jnp.arange(points, dtype=jnp.int32).astype(jnp.float32)
    within = jnp.arange(block, dtype=jnp.int32)

    def degrid_visit(carry, inputs):
        position, coord_block, obs_block = inputs
        turns = along[:, None] * coord_block[None, :] / points
        fraction = turns - jnp.floor(turns)
        cosine = jnp.cos(TWO_PI * fraction)
        sine = jnp.sin(TWO_PI * fraction)
        degrid_table = jnp.concatenate(
            [jnp.concatenate([cosine, sine], 1), jnp.concatenate([-sine, cosine], 1)], 0
        ).astype(jnp.bfloat16)
        model = product(grid, degrid_table) / math.sqrt(points)
        live = (position * block + within < live_count) & is_held
        resid_re = jnp.where(live[None, :], obs_block[0] - model[:, :block], jnp.float32(0.0))
        resid_im = jnp.where(live[None, :], obs_block[1] - model[:, block:], jnp.float32(0.0))
        residual = jnp.concatenate([resid_re, resid_im], -1).astype(jnp.bfloat16)
        carry = carry + product(residual, degrid_table.T)
        return (carry, residual)

    initial = jnp.zeros((strip_rows, 2 * points), jnp.float32)
    total_sum, residuals = lax.scan(
        degrid_visit, initial, (jnp.arange(blocks, dtype=jnp.int32), coord_blocks, obs_blocks)
    )
    update = (total_sum / math.sqrt(total)).astype(jnp.bfloat16)
    resid_re = residuals[..., :block].transpose(1, 0, 2).reshape(strip_rows, total)
    resid_im = residuals[..., block:].transpose(1, 0, 2).reshape(strip_rows, total)
    return (update, jnp.stack([resid_re, resid_im], 0))


def lift_back(updates, slot_ids, offsets, anchor, phase_table, modulus, points, product):
    number = updates.shape[0]
    strip_rows = updates.shape[1]
    subgrid_count = offsets.shape[0]
    chosen = jnp.sum(
        jnp.where(
            slot_ids[:, None] == jnp.arange(subgrid_count, dtype=jnp.int32)[None, :],
            offsets[None, :],
            0,
        ),
        axis=1,
    )
    along = jnp.arange(points, dtype=jnp.int32)
    cosine, sine = phasor(
        modular_product(anchor, (along[None, :] + chosen[:, None]) % modulus, modulus), modulus
    )
    upd_re = updates[..., :points].astype(jnp.float32)
    upd_im = updates[..., points:].astype(jnp.float32)
    lift_re = upd_re * cosine[:, None] - upd_im * sine[:, None]
    lift_im = upd_re * sine[:, None] + upd_im * cosine[:, None]
    lifted = (
        jnp.concatenate([lift_re, lift_im], -1)
        .astype(jnp.bfloat16)
        .reshape(number * strip_rows, 2 * points)
    )
    width = phase_table.shape[0] // 2
    back = product(lifted, phase_table.T).reshape(number, strip_rows, 2 * width)
    across = jnp.arange(width, dtype=jnp.int32)
    col_cos, col_sin = phasor(modular_product(across[None, :], chosen[:, None], modulus), modulus)
    back_re = back[..., :width]
    back_im = back[..., width:]
    out_re = jnp.sum(back_re * col_cos[:, None] - back_im * col_sin[:, None], axis=0)
    out_im = jnp.sum(back_re * col_sin[:, None] + back_im * col_cos[:, None], axis=0)
    return jnp.concatenate([out_re, out_im], -1)


def local(sky_strips, prolate, subgrid_offset, owner, observed, vis_uv, vis_count):
    width = sky_strips.shape[2]
    strip_rows = sky_strips.shape[1]
    facets = lax.axis_size("facet")
    my_index = lax.axis_index("facet")
    modulus = width * facets
    slots = observed.shape[0]
    subgrid_count = owner.shape[0]
    phase_table = forward_table(width, POINTS, modulus)
    columns = jnp.arange(width, dtype=jnp.int32)
    anchor = my_index * width
    strip_re = sky_strips[0].astype(jnp.float32)
    strip_im = sky_strips[1].astype(jnp.float32)
    slot_ids, is_held = slot_layout(owner, slots, slots * facets)
    my_held = lax.dynamic_slice_in_dim(is_held, my_index * slots, slots)
    count = subgrid_count * strip_rows
    number = count // strip_rows
    terms = facet_terms(
        strip_re,
        strip_im,
        prolate,
        columns,
        anchor,
        subgrid_offset,
        phase_table,
        modulus,
        POINTS,
        local_product,
    )
    terms = terms.reshape(count, 2 * POINTS).reshape(subgrid_count, strip_rows * 2 * POINTS)
    outgoing = jnp.where(
        is_held[:, None], jnp.take(terms, slot_ids, axis=0), jnp.float32(0.0)
    ).reshape(facets, slots, strip_rows * 2 * POINTS)
    incoming = lax.all_to_all(
        outgoing.astype(jnp.bfloat16), "facet", split_axis=0, concat_axis=0, tiled=True
    ).astype(outgoing.dtype)
    grids = jnp.sum(incoming, axis=0).astype(jnp.bfloat16).reshape(slots, strip_rows, 2 * POINTS)
    block = min(1024, observed.shape[3])
    update_list = []
    residual_list = []
    for position in range(slots):
        update, residual = degrid_slot(
            grids[position],
            observed[position],
            vis_uv[position],
            vis_count[position],
            my_held[position],
            block,
            POINTS,
            local_product,
        )
        update_list.append(update)
        residual_list.append(residual)
    updates = jnp.stack(update_list, 0)
    residual_vis = jnp.stack(residual_list, 0)

    def add_slots(total, piece):
        number = piece.shape[0]
        group_size = 64
        if number > group_size and number % group_size == 0:
            grouped = piece.reshape(number // group_size, group_size, strip_rows, 2 * POINTS)
            id_groups = slot_ids.reshape(number // group_size, group_size)

            def add_visit(running, inputs):
                return (
                    running
                    + lift_back(
                        inputs[0],
                        inputs[1],
                        subgrid_offset,
                        anchor,
                        phase_table,
                        modulus,
                        POINTS,
                        local_product,
                    ),
                    None,
                )

            running, _ = lax.scan(add_visit, total, (grouped, id_groups))
            return running
        return total + lift_back(
            piece, slot_ids, subgrid_offset, anchor, phase_table, modulus, POINTS, local_product
        )

    empty_image = jnp.zeros((strip_rows, 2 * width), jnp.float32)
    back_sum = add_slots(empty_image, lax.all_gather(updates, "facet", axis=0, tiled=True))
    weight = jnp.concatenate([prolate, prolate]) / math.sqrt(subgrid_count * POINTS)
    image_update = (back_sum * weight).reshape(strip_rows, 2, width).transpose(1, 0, 2)
    return (residual_vis, image_update)


def solution(mesh):
    in_specs = (
        P(None, "groups", "facet"),
        P(),
        P(),
        P(),
        P(("groups", "facet"), None, None, None),
        P(("groups", "facet"), None),
        P(("groups", "facet")),
    )
    out_specs = (P(("groups", "facet"), None, None, None), P(None, "groups", "facet"))
    return jax.shard_map(local, mesh=mesh, in_specs=in_specs, out_specs=out_specs, check_vma=False)
```

profile of v0, /device:TPU:0, one launch (start us, length us, event | category | flops | bytes accessed | tf_op | source)
XLA Modules:
  0.0 340.6 jit_solution(12584990925664134478)
XLA Ops:
  4.1 11.1 %negate_convert_fusion.2 = (bf16[1024,512]{1,0:T(8,128)(2,1)S(1)}, bf16[1024,512]{1,0:T(8,128)(2,1)S(1)}, bf16[1024,512]{1,0:T(8,128)(2,1)S(1)}) fusion(s32[512]{0:T(512)S(1)} %get-tuple-element.333, s32[512]{0:T(512)S(1)} %get-tuple-element.334), kind=kLoop, calls=%fused_computation.96 | loop fusion | flops 28311552 | bytes 3149824 | tf_op jit(solution)/shard_map/convert.32
  18.6 1.6 select_convert_fusion
  20.1 7.6 %all-to-all-start = ((bf16[16,2,8192]{2,1,0:T(2,128)(2,1)}), bf16[16,2,8192]{2,1,0:T(2,128)(2,1)S(1)}, u32[]{:S(2)}, u32[]{:S(2)}) async-start(bf16[16,2,8192]{2,1,0:T(2,128)(2,1)} %select_convert_fusion), calls=%async_computation | async-start | bytes 1048576 | tf_op jit(solution)/shard_map/all_to_all | solution.py:184
  34.0 1.5 fusion.101
  35.5 6.5 %all-to-all-done = bf16[16,2,8192]{2,1,0:T(2,128)(2,1)S(1)} async-done(((bf16[16,2,8192]{2,1,0:T(2,128)(2,1)}), bf16[16,2,8192]{2,1,0:T(2,128)(2,1)S(1)}, u32[]{:S(2)}, u32[]{:S(2)}) %all-to-all-start) | async-done | bytes 524320 | tf_op jit(solution)/shard_map/all_to_all | solution.py:184
  43.7 139.2 %while.27 = (s32[]{:T(128)}, f32[8,1024]{1,0:T(8,128)}, bf16[8,8,2048]{2,1,0:T(8,128)(2,1)S(1)}, s32[8]{0:T(128)}, s32[]{:T(128)}, /*index=5*/pred[]{:T(512)}, f...) while((s32[]{:T(128)}, f32[8,1024]{1,0:T(8,128)}, ...), condition=%wide.region_7.8_spmd.clone, body=%wide.region_6.7_spmd.clone.sunk | while | flops 105598464 | bytes 9996492 | solution.py:106
  44.5 8.6 %fusion.178 = (bf16[512,1024]{1,0:T(8,128)(2,1)S(1)}, bf16[512,1024]{1,0:T(8,128)(2,1)S(1)}, bf16[512,1024]{1,0:T(8,128)(2,1)S(1)}) fusion(f32[1024]{0:T(1024)S(1)} %bitcast.135, f32[512]{0:T(512)S(1)} %iota_convert_fusion.5), kind=kLoop, calls=%fused_computation.45.clone.1 | loop fusion | flops 4718592 | bytes 3151872 | tf_op jit(solution)/shard_map/convert.24
  53.1 1.4 fusion.179
  58.7 1.8 fusion.182
  61.2 8.6 %fusion.178 = (bf16[512,1024]{1,0:T(8,128)(2,1)S(1)}, bf16[512,1024]{1,0:T(8,128)(2,1)S(1)}, bf16[512,1024]{1,0:T(8,128)(2,1)S(1)}) fusion(f32[1024]{0:T(1024)S(1)} %bitcast.135, f32[512]{0:T(512)S(1)} %iota_convert_fusion.5), kind=kLoop, calls=%fused_computation.45.clone.1 | loop fusion | flops 4718592 | bytes 3151872 | tf_op jit(solution)/shard_map/convert.24
  69.8 1.4 fusion.179
  75.4 2.6 fusion.182
  78.7 8.6 %fusion.178 = (bf16[512,1024]{1,0:T(8,128)(2,1)S(1)}, bf16[512,1024]{1,0:T(8,128)(2,1)S(1)}, bf16[512,1024]{1,0:T(8,128)(2,1)S(1)}) fusion(f32[1024]{0:T(1024)S(1)} %bitcast.135, f32[512]{0:T(512)S(1)} %iota_convert_fusion.5), kind=kLoop, calls=%fused_computation.45.clone.1 | loop fusion | flops 4718592 | bytes 3151872 | tf_op jit(solution)/shard_map/convert.24
  87.3 1.4 fusion.179
  92.9 2.6 fusion.182
  96.2 8.6 %fusion.178 = (bf16[512,1024]{1,0:T(8,128)(2,1)S(1)}, bf16[512,1024]{1,0:T(8,128)(2,1)S(1)}, bf16[512,1024]{1,0:T(8,128)(2,1)S(1)}) fusion(f32[1024]{0:T(1024)S(1)} %bitcast.135, f32[512]{0:T(512)S(1)} %iota_convert_fusion.5), kind=kLoop, calls=%fused_computation.45.clone.1 | loop fusion | flops 4718592 | bytes 3151872 | tf_op jit(solution)/shard_map/convert.24
  104.8 1.4 fusion.179
  110.4 2.6 fusion.182
  113.7 8.6 %fusion.178 = (bf16[512,1024]{1,0:T(8,128)(2,1)S(1)}, bf16[512,1024]{1,0:T(8,128)(2,1)S(1)}, bf16[512,1024]{1,0:T(8,128)(2,1)S(1)}) fusion(f32[1024]{0:T(1024)S(1)} %bitcast.135, f32[512]{0:T(512)S(1)} %iota_convert_fusion.5), kind=kLoop, calls=%fused_computation.45.clone.1 | loop fusion | flops 4718592 | bytes 3151872 | tf_op jit(solution)/shard_map/convert.24
  122.3 1.4 fusion.179
  127.9 2.6 fusion.182
  131.2 8.6 %fusion.178 = (bf16[512,1024]{1,0:T(8,128)(2,1)S(1)}, bf16[512,1024]{1,0:T(8,128)(2,1)S(1)}, bf16[512,1024]{1,0:T(8,128)(2,1)S(1)}) fusion(f32[1024]{0:T(1024)S(1)} %bitcast.135, f32[512]{0:T(512)S(1)} %iota_convert_fusion.5), kind=kLoop, calls=%fused_computation.45.clone.1 | loop fusion | flops 4718592 | bytes 3151872 | tf_op jit(solution)/shard_map/convert.24
  139.8 1.4 fusion.179
  145.4 2.6 fusion.182
  148.7 8.6 %fusion.178 = (bf16[512,1024]{1,0:T(8,128)(2,1)S(1)}, bf16[512,1024]{1,0:T(8,128)(2,1)S(1)}, bf16[512,1024]{1,0:T(8,128)(2,1)S(1)}) fusion(f32[1024]{0:T(1024)S(1)} %bitcast.135, f32[512]{0:T(512)S(1)} %iota_convert_fusion.5), kind=kLoop, calls=%fused_computation.45.clone.1 | loop fusion | flops 4718592 | bytes 3151872 | tf_op jit(solution)/shard_map/convert.24
  157.3 1.4 fusion.179
  162.9 2.6 fusion.182
  166.2 8.6 %fusion.178 = (bf16[512,1024]{1,0:T(8,128)(2,1)S(1)}, bf16[512,1024]{1,0:T(8,128)(2,1)S(1)}, bf16[512,1024]{1,0:T(8,128)(2,1)S(1)}) fusion(f32[1024]{0:T(1024)S(1)} %bitcast.135, f32[512]{0:T(512)S(1)} %iota_convert_fusion.5), kind=kLoop, calls=%fused_computation.45.clone.1 | loop fusion | flops 4718592 | bytes 3151872 | tf_op jit(solution)/shard_map/convert.24
  174.8 1.4 fusion.179
  180.4 2.6 fusion.182
  184.3 128.4 %while.26 = (s32[]{:T(128)}, f32[8,1024]{1,0:T(8,128)}, bf16[8,8,2048]{2,1,0:T(8,128)(2,1)S(1)}, s32[8]{0:T(128)S(1)}, s32[]{:T(128)}, /*index=5*/pred[]{:T(512)...) while((s32[]{:T(128)}, f32[8,1024]{1,0:T(8,128)}, ...), condition=%wide.region_5.6_spmd.clone, body=%wide.region_4.5_spmd.clone.sunk | while | flops 105598464 | bytes 9996492 | solution.py:106
  184.3 8.6 %fusion.171 = (bf16[512,1024]{1,0:T(8,128)(2,1)S(1)}, bf16[512,1024]{1,0:T(8,128)(2,1)S(1)}, bf16[512,1024]{1,0:T(8,128)(2,1)S(1)}) fusion(f32[1024]{0:T(1024)S(1)} %bitcast.136, f32[512]{0:T(512)S(1)} %iota_convert_fusion.4), kind=kLoop, calls=%fused_computation.13.clone.1 | loop fusion | flops 4718592 | bytes 3151872 | tf_op jit(solution)/shard_map/convert.12
  192.9 1.4 fusion.172
  196.5 1.3 fusion.173
  197.9 1.8 fusion.175
  199.7 8.6 %fusion.171 = (bf16[512,1024]{1,0:T(8,128)(2,1)S(1)}, bf16[512,1024]{1,0:T(8,128)(2,1)S(1)}, bf16[512,1024]{1,0:T(8,128)(2,1)S(1)}) fusion(f32[1024]{0:T(1024)S(1)} %bitcast.136, f32[512]{0:T(512)S(1)} %iota_convert_fusion.4), kind=kLoop, calls=%fused_computation.13.clone.1 | loop fusion | flops 4718592 | bytes 3151872 | tf_op jit(solution)/shard_map/convert.12
  208.3 1.4 fusion.172
  211.9 1.3 fusion.173
  213.3 2.6 fusion.175
  215.9 8.6 %fusion.171 = (bf16[512,1024]{1,0:T(8,128)(2,1)S(1)}, bf16[512,1024]{1,0:T(8,128)(2,1)S(1)}, bf16[512,1024]{1,0:T(8,128)(2,1)S(1)}) fusion(f32[1024]{0:T(1024)S(1)} %bitcast.136, f32[512]{0:T(512)S(1)} %iota_convert_fusion.4), kind=kLoop, calls=%fused_computation.13.clone.1 | loop fusion | flops 4718592 | bytes 3151872 | tf_op jit(solution)/shard_map/convert.12
  224.4 1.4 fusion.172
  228.1 1.3 fusion.173
  229.4 2.6 fusion.175
  232.0 8.6 %fusion.171 = (bf16[512,1024]{1,0:T(8,128)(2,1)S(1)}, bf16[512,1024]{1,0:T(8,128)(2,1)S(1)}, bf16[512,1024]{1,0:T(8,128)(2,1)S(1)}) fusion(f32[1024]{0:T(1024)S(1)} %bitcast.136, f32[512]{0:T(512)S(1)} %iota_convert_fusion.4), kind=kLoop, calls=%fused_computation.13.clone.1 | loop fusion | flops 4718592 | bytes 3151872 | tf_op jit(solution)/shard_map/convert.12
  240.6 1.4 fusion.172
  244.2 1.3 fusion.173
  245.6 2.6 fusion.175
  248.1 8.6 %fusion.171 = (bf16[512,1024]{1,0:T(8,128)(2,1)S(1)}, bf16[512,1024]{1,0:T(8,128)(2,1)S(1)}, bf16[512,1024]{1,0:T(8,128)(2,1)S(1)}) fusion(f32[1024]{0:T(1024)S(1)} %bitcast.136, f32[512]{0:T(512)S(1)} %iota_convert_fusion.4), kind=kLoop, calls=%fused_computation.13.clone.1 | loop fusion | flops 4718592 | bytes 3151872 | tf_op jit(solution)/shard_map/convert.12
  256.7 1.4 fusion.172
  260.3 1.3 fusion.173
  261.7 2.6 fusion.175
  264.3 8.6 %fusion.171 = (bf16[512,1024]{1,0:T(8,128)(2,1)S(1)}, bf16[512,1024]{1,0:T(8,128)(2,1)S(1)}, bf16[512,1024]{1,0:T(8,128)(2,1)S(1)}) fusion(f32[1024]{0:T(1024)S(1)} %bitcast.136, f32[512]{0:T(512)S(1)} %iota_convert_fusion.4), kind=kLoop, calls=%fused_computation.13.clone.1 | loop fusion | flops 4718592 | bytes 3151872 | tf_op jit(solution)/shard_map/convert.12
  272.9 1.4 fusion.172
  276.5 1.3 fusion.173
  277.9 2.6 fusion.175
  280.4 8.6 %fusion.171 = (bf16[512,1024]{1,0:T(8,128)(2,1)S(1)}, bf16[512,1024]{1,0:T(8,128)(2,1)S(1)}, bf16[512,1024]{1,0:T(8,128)(2,1)S(1)}) fusion(f32[1024]{0:T(1024)S(1)} %bitcast.136, f32[512]{0:T(512)S(1)} %iota_convert_fusion.4), kind=kLoop, calls=%fused_computation.13.clone.1 | loop fusion | flops 4718592 | bytes 3151872 | tf_op jit(solution)/shard_map/convert.12
  289.0 1.4 fusion.172
  292.6 1.3 fusion.173
  294.0 2.6 fusion.175
  296.6 8.6 %fusion.171 = (bf16[512,1024]{1,0:T(8,128)(2,1)S(1)}, bf16[512,1024]{1,0:T(8,128)(2,1)S(1)}, bf16[512,1024]{1,0:T(8,128)(2,1)S(1)}) fusion(f32[1024]{0:T(1024)S(1)} %bitcast.136, f32[512]{0:T(512)S(1)} %iota_convert_fusion.4), kind=kLoop, calls=%fused_computation.13.clone.1 | loop fusion | flops 4718592 | bytes 3151872 | tf_op jit(solution)/shard_map/convert.12
  305.2 1.4 fusion.172
  310.1 2.6 fusion.175
  314.5 21.3 %all_gather.3 = bf16[32,8,1024]{2,1,0:T(8,128)(2,1)S(1)} all-gather(bf16[2,8,1024]{2,1,0:T(8,128)(2,1)S(1)} %pad_maximum_fusion.2), channel_id=1, replica_groups=mesh['groups'=2,'facet'=16] {'facet'}, dimensions={0}, use_global_device_ids=true | all-gather | bytes 557056 | tf_op jit(solution)/shard_map/all_gather | solution.py:237
  337.9 1.3 fusion.44
  (195 shorter events, 70.6 us)
Async XLA Ops:
  0.6 15.1 %copy-start.14 = (f32[1024]{0:T(1024)S(1)}, f32[1024]{0:T(1024)}, u32[]{:S(2)}) copy-start(f32[1024]{0:T(1024)} %param.12) | copy-start | bytes 12292
  0.6 15.1 %copy-start.12 = (bf16[2,8,1024]{2,1,0:T(8,128)(2,1)S(1)}, bf16[2,8,1024]{2,1,0:T(8,128)(2,1)}, u32[]{:S(2)}) copy-start(bf16[2,8,1024]{2,1,0:T(8,128)(2,1)} %param.11) | copy-start | bytes 98308
  15.3 1.3 copy-start.1
  15.3 1.3 copy-start.3
  15.3 1.6 copy-start.5
  18.1 9.7 %copy-start = (f32[2,2,8,8192]{3,2,1,0:T(8,128)S(1)}, f32[2,2,8,8192]{3,2,1,0:T(8,128)}, u32[]{:S(2)}) copy-start(f32[2,2,8,8192]{3,2,1,0:T(8,128)} %param.15) | copy-start | bytes 3145732
  20.1 8.8 %copy-start.11 = (f32[2,8192]{1,0:T(2,128)S(1)}, f32[2,8192]{1,0:T(2,128)}, u32[]{:S(2)}) copy-start(f32[2,8192]{1,0:T(2,128)} %param.16) | copy-start | bytes 196612
  20.1 21.8 %all-to-all-start = ((bf16[16,2,8192]{2,1,0:T(2,128)(2,1)}), bf16[16,2,8192]{2,1,0:T(2,128)(2,1)S(1)}, u32[]{:S(2)}, u32[]{:S(2)}) async-start(bf16[16,2,8192]{2,1,0:T(2,128)(2,1)} %select_convert_fusion), calls=%async_computation | async-start | bytes 1048576 | tf_op jit(solution)/shard_map/all_to_all | solution.py:184
  27.8 3.7 %copy-start.15 = (s32[2]{0:T(128)S(1)}, s32[2]{0:T(128)}, u32[]{:S(2)}) copy-start(s32[2]{0:T(128)} %param.17) | copy-start | bytes 28
  27.8 5.0 %copy-start.16 = (s32[16]{0:T(128)S(1)}, s32[16]{0:T(128)}, u32[]{:S(2)}) copy-start(s32[16]{0:T(128)} %param.13) | copy-start | bytes 196
  312.7 25.0 %copy-start.9 = (f32[32,512]{1,0:T(8,128)S(1)}, f32[32,512]{1,0:T(8,128)}, u32[]{:S(2)}) copy-start(f32[32,512]{1,0:T(8,128)} %get-tuple-element.323) | copy-start | bytes 196612
  312.7 25.0 %copy-start.10 = (f32[32,512]{1,0:T(8,128)S(1)}, f32[32,512]{1,0:T(8,128)}, u32[]{:S(2)}) copy-start(f32[32,512]{1,0:T(8,128)} %get-tuple-element.324) | copy-start | bytes 196612
  312.7 25.1 %copy-start.2 = (bf16[1024,512]{1,0:T(8,128)(2,1)S(1)}, bf16[1024,512]{1,0:T(8,128)(2,1)}, u32[]{:S(2)}) copy-start(bf16[1024,512]{1,0:T(8,128)(2,1)} %copy-done.1) | copy-start | bytes 3145732
  312.8 25.1 %copy-start.4 = (bf16[1024,512]{1,0:T(8,128)(2,1)S(1)}, bf16[1024,512]{1,0:T(8,128)(2,1)}, u32[]{:S(2)}) copy-start(bf16[1024,512]{1,0:T(8,128)(2,1)} %copy-done.3) | copy-start | bytes 3145732
  312.8 25.1 %copy-start.6 = (bf16[1024,512]{1,0:T(8,128)(2,1)S(1)}, bf16[1024,512]{1,0:T(8,128)(2,1)}, u32[]{:S(2)}) copy-start(bf16[1024,512]{1,0:T(8,128)(2,1)} %copy-done.5) | copy-start | bytes 3145732
  337.9 1.4 copy-start.7
  337.9 1.4 copy-start.8
  339.2 0.7 copy-start.13
where the time goes:
time: 344 us; the launch traced here: 341 us
  other arithmetic  183 us (53%)
  matrix products  63.4 us (18%)
  local copies, waits for them, and re-layouts  47.8 us (14%)
  blocking collectives  21.3 us (6%)
  loops' own time  10.2 us (3%)
  starting transfers between devices  7.55 us (2%)
  waiting for transfers between devices  6.49 us (2%)
    another operation x35, other arithmetic  149 us
    dot_general x34, matrix products, local_product(): return jnp.dot(first, second, preferred_element_type=jnp.float32)  63.4 us
    all_gather x1, blocking collectives, local(): lax.all_gather(updates, 'facet', axis=0, tiled=True)  21.3 us
    dynamic_slice x32, local copies, waits for them, and re-layouts, degrid_slot(): lax.scan(degrid_visit, initial, (jnp.arange(blocks, dtype=jnp.int32), coo...  20.6 us
    and x16, other arithmetic, degrid_visit(): live = (position * block + within < live_count) & is_held  20.3 us
    slice x16, local copies, waits for them, and re-layouts, degrid_visit(): obs_block[0] - model[:, :block]  17.3 us
    another operation x2, loops' own time, degrid_slot(): lax.scan(degrid_visit, initial, (jnp.arange(blocks, dtype=jnp.int32), coo...  10.2 us
    all_to_all x1, starting transfers between devices, local(): lax.all_to_all(outgoing.astype(jnp.bfloat16), 'facet', split_axis=0, conc...  7.55 us
  transfers between devices with their start and end apart: 1, of which 1 were waited for; matrix products, arithmetic and copies ran while one was open for 2% of the time, Pallas kernels for 0%

commit v1 on v0

v1 whole, which is shorter than its diff:
```python
import functools
import math

import jax
import jax.numpy as jnp
from jax import lax
from jax.experimental import pallas as pl
from jax.experimental.pallas import tpu as pltpu
from jax.sharding import PartitionSpec as P

POINTS = 512
FINE = 8
COARSE = POINTS // FINE
BLOCK = 2 * COARSE
ROOT = 8
STEP = 64
CHUNK = 1024

COS = (
    0.9999999890590217, -4.934801124863452, 4.058694841243232, -1.3351584301691248,
    0.23502980840046309, -0.025358983639642813, 0.001593910683444594,
)
SIN = (
    3.14159265125575, -5.167712550664621, 2.550160355805489, -0.5992423074495862,
    0.08208188864038139, -0.00727531575291481, 0.00039528045693413335,
)


def horner(coefficients, z):
    total = coefficients[-1] * z + coefficients[-2]
    for value in coefficients[-3::-1]:
        total = total * z + value
    return total


def turn(t):
    y = 2.0 * (t - jnp.floor(t + 0.5))
    z = y * y
    return horner(COS, z), horner(SIN, z) * y


def modular(first, second, modulus):
    if modulus & (modulus - 1) == 0:
        return (first * second) & (modulus - 1)
    upper = second // 256
    lower = second % 256
    return (first * lower % modulus + first * upper % modulus * 256 % modulus) % modulus


def iota(shape, axis):
    return lax.broadcasted_iota(jnp.int32, shape, axis)


def column_points(shape):
    column = iota(shape, 1)
    return (column % COARSE) * FINE + column // BLOCK, (column // COARSE) % 2


def facet_at(position, me, facets):
    bits = facets.bit_length() - 1
    flipped = position * 0
    for bit in range(bits):
        flipped = flipped | (((position >> bit) & 1) << (bits - 1 - bit))
    return flipped ^ me


def swap(block):
    return pltpu.roll(block, COARSE, 1)


def blocks_of(value):
    return [value[:, b * BLOCK : (b + 1) * BLOCK] for b in range(FINE)]


def prepare_kernel(modulus, slots, uv_ref, table_ref, coarse_ref, fine_ref, v_re, v_im, u_re, u_im):
    width = table_ref.shape[0] // 2
    points, part = column_points(v_re.shape)
    fraction = modular(iota(v_re.shape, 0), points, modulus).astype(jnp.float32) * (1.0 / modulus)
    v_re[...], v_im[...] = turn(fraction + 0.25 * part.astype(jnp.float32))
    points, _ = column_points(u_re.shape)
    fraction = modular(iota(u_re.shape, 0) * STEP, points, modulus).astype(jnp.float32) * (1.0 / modulus)
    u_re[...], u_im[...] = turn(fraction)

    def table_step(step, _):
        c = u_re[pl.ds(step, 1), :]
        s = u_im[pl.ds(step, 1), :]
        row = pl.multiple_of(step * STEP, STEP)
        table_ref[pl.ds(row, STEP), :] = (v_re[...] * c - v_im[...] * s).astype(jnp.bfloat16)
        table_ref[pl.ds(width + row, STEP), :] = (v_re[...] * s + v_im[...] * c).astype(jnp.bfloat16)
        return 0

    lax.fori_loop(0, width // STEP, table_step, 0)

    total = uv_ref.shape[1]
    chunk = min(512, total)

    for slot in range(slots):

        def coarse_step(step, _):
            at = pl.ds(pl.multiple_of(step * chunk, chunk), chunk)
            u = jnp.broadcast_to(uv_ref[slot : slot + 1, at], (ROOT, chunk))
            fine = u * (1.0 / POINTS)
            fine_ref[slot, 0, :, at], fine_ref[slot, 1, :, at] = turn(fine)
            low = u * (FINE / POINTS)
            low = low - jnp.floor(low)
            re, im = turn(low * iota(u.shape, 0).astype(jnp.float32))
            c, s = turn(u * (FINE * ROOT / POINTS))
            for pair in range(ROOT // 2):
                next_re = re * c - im * s
                next_im = re * s + im * c
                rows = pair * 2 * ROOT
                coarse_ref[slot, rows : rows + 2 * ROOT, at] = jnp.concatenate(
                    [re, next_re], 0
                ).astype(jnp.bfloat16)
                coarse_ref[slot, COARSE + rows : COARSE + rows + 2 * ROOT, at] = jnp.concatenate(
                    [im, next_im], 0
                ).astype(jnp.bfloat16)
                re = next_re * c - next_im * s
                im = next_re * s + next_im * c
            return 0

        lax.fori_loop(0, total // chunk, coarse_step, 0)


def visibility_kernel(
    modulus,
    facets,
    me_ref,
    owner_ref,
    offset_ref,
    count_ref,
    sky_ref,
    prolate_ref,
    table_ref,
    coarse_ref,
    fine_ref,
    observed_ref,
    residual_ref,
    update_ref,
    lhs,
    raw,
    mod_c,
    mod_s,
    turn_c,
    turn_s,
):
    me = me_ref[0]
    slots = count_ref.shape[0]
    rows = sky_ref.shape[2]
    width = sky_ref.shape[3]
    subgrids = owner_ref.shape[0]

    def find(index, carry):
        held, offsets = carry
        mine = owner_ref[index] == me
        offsets = tuple(
            jnp.where(mine & (held == slot), offset_ref[index], offsets[slot]) for slot in range(slots)
        )
        return held + mine.astype(jnp.int32), offsets

    zero = jnp.int32(0)
    held, offsets = lax.fori_loop(0, subgrids, find, (zero, (zero,) * slots))

    facet = facet_at(iota((facets, width), 0), me, facets)
    across = facet * width + iota((facets, width), 1)
    for slot in range(slots):
        fraction = modular(across, offsets[slot], modulus).astype(jnp.float32) * (1.0 / modulus)
        c, s = turn(fraction)
        mod_c[slot] = c * prolate_ref[...]
        mod_s[slot] = s * prolate_ref[...]

    points, part = column_points((facets, FINE * BLOCK))
    facet = facet_at(iota(points.shape, 0), me, facets)
    c, s = turn(modular(facet, points, facets).astype(jnp.float32) * (1.0 / facets))
    scale = 1.0 / math.sqrt(modulus)
    turn_c[...] = c * scale
    turn_s[...] = jnp.where(part == 0, -s, s) * scale

    for slot in range(slots):

        def modulate(pair, _):
            parts = []
            for which in range(2):
                position = pair * 2 + which
                c = mod_c[slot, pl.ds(position, 1), :]
                s = mod_s[slot, pl.ds(position, 1), :]
                re = sky_ref[position, 0].astype(jnp.float32)
                im = sky_ref[position, 1].astype(jnp.float32)
                parts.append((re * c + im * s, im * c - re * s))
            row = pl.multiple_of((slot * facets + pair * 2) * rows, 2 * rows)
            at = pl.ds(row, 2 * rows)
            lhs[at, :width] = jnp.concatenate([parts[0][0], parts[1][0]], 0).astype(jnp.bfloat16)
            lhs[at, width:] = jnp.concatenate([parts[0][1], parts[1][1]], 0).astype(jnp.bfloat16)
            return 0

        lax.fori_loop(0, facets // 2, modulate, 0)

    raw[...] = jnp.dot(lhs[...], table_ref[...], preferred_element_type=jnp.float32)

    total = observed_ref.shape[3]
    chunk = min(CHUNK, total)
    first_half = jnp.where(iota((rows, BLOCK), 1) < COARSE, jnp.float32(1.0), jnp.float32(-1.0))

    for slot in range(slots):

        def add_facet(position, carry):
            straight, crossed = carry
            row = pl.multiple_of((slot * facets + position) * rows, rows)
            value = raw[pl.ds(row, rows), :]
            return (
                straight + value * turn_c[pl.ds(position, 1), :],
                crossed + value * turn_s[pl.ds(position, 1), :],
            )

        empty = jnp.zeros((rows, FINE * BLOCK), jnp.float32)
        straight, crossed = lax.fori_loop(0, facets, add_facet, (empty, empty))
        grid = [
            (first + swap(second)).astype(jnp.bfloat16).astype(jnp.float32)
            for first, second in zip(blocks_of(straight), blocks_of(crossed))
        ]
        points_lhs = jnp.concatenate(
            [block * first_half for block in grid] + [swap(block) for block in grid], 0
        ).astype(jnp.bfloat16)
        live = jnp.where(slot < held, count_ref[slot], 0)

        def visit(step, carry):
            at = pl.ds(pl.multiple_of(step * chunk, chunk), chunk)
            coarse = coarse_ref[slot, :, at]
            c = fine_ref[slot, 0, :, at]
            s = fine_ref[slot, 1, :, at]
            terms = jnp.dot(points_lhs, coarse, preferred_element_type=jnp.float32)
            half = FINE * rows
            re = terms[half - rows : half]
            im = terms[2 * half - rows :]
            for b in range(FINE - 2, -1, -1):
                re, im = (
                    terms[b * rows : (b + 1) * rows] + (re * c - im * s),
                    terms[half + b * rows : half + (b + 1) * rows] + (re * s + im * c),
                )
            scale = 1.0 / math.sqrt(POINTS)
            alive = step * chunk + iota((rows, chunk), 1) < live
            re = jnp.where(alive, observed_ref[slot, 0, :, at] - re * scale, 0.0).astype(jnp.bfloat16)
            im = jnp.where(alive, observed_ref[slot, 1, :, at] - im * scale, 0.0).astype(jnp.bfloat16)
            residual_ref[slot, 0, :, at] = re
            residual_ref[slot, 1, :, at] = im
            re = re.astype(jnp.float32)
            im = im.astype(jnp.float32)
            all_re, all_im = [re], [im]
            for b in range(1, FINE):
                re, im = re * c + im * s, im * c - re * s
                all_re.append(re)
                all_im.append(im)
            spread = jnp.concatenate(all_re + all_im, 0).astype(jnp.bfloat16)
            return carry + lax.dot_general(
                spread, coarse, (((1,), (1,)), ((), ())), preferred_element_type=jnp.float32
            )

        gathered = lax.fori_loop(
            0, total // chunk, visit, jnp.zeros((2 * FINE * rows, BLOCK), jnp.float32)
        )
        scale = 1.0 / math.sqrt(total)
        for b in range(FINE):
            re = gathered[b * rows : (b + 1) * rows]
            im = gathered[(FINE + b) * rows : (FINE + b + 1) * rows]
            update_ref[slot, :, b * BLOCK : (b + 1) * BLOCK] = (
                (swap(im) + re * first_half) * scale
            ).astype(jnp.bfloat16)


def image_kernel(
    modulus,
    facets,
    slots,
    me_ref,
    owner_ref,
    offset_ref,
    update_ref,
    prolate_ref,
    table_ref,
    image_ref,
    lhs,
    mod_c,
    mod_s,
    taken,
    place,
):
    me = me_ref[0]
    subgrids = owner_ref.shape[0]
    rows = update_ref.shape[1]
    width = image_ref.shape[2]

    def clear(index, _):
        taken[index] = 0
        return 0

    lax.fori_loop(0, facets, clear, 0)

    def assign(index, _):
        holder = owner_ref[index]
        rank = taken[holder]
        taken[holder] = rank + 1
        place[index] = facet_at(holder ^ me, 0, facets) * slots + rank
        return 0

    lax.fori_loop(0, subgrids, assign, 0)

    across = me * width + iota((subgrids, width), 1)
    fraction = modular(across, jnp.broadcast_to(offset_ref[...], across.shape), modulus)
    mod_c[...], mod_s[...] = turn(fraction.astype(jnp.float32) * (1.0 / modulus))

    points, part = column_points((rows, FINE * BLOCK))
    straight, crossed = turn(modular(me, points, facets).astype(jnp.float32) * (1.0 / facets))
    crossed = jnp.where(part == 0, -crossed, crossed)

    def lift(pair, _):
        parts = []
        for which in range(2):
            value = update_ref[place[pair * 2 + which]].astype(jnp.float32)
            turned = jnp.concatenate([swap(block) for block in blocks_of(value)], 1)
            parts.append(value * straight + turned * crossed)
        at = pl.ds(pl.multiple_of(pair * 2 * rows, 2 * rows), 2 * rows)
        lhs[at, :] = jnp.concatenate(parts, 0).astype(jnp.bfloat16)
        return 0

    lax.fori_loop(0, subgrids // 2, lift, 0)
    back = lax.dot_general(
        lhs[...], table_ref[...], (((1,), (1,)), ((), ())), preferred_element_type=jnp.float32
    )
    out_re = jnp.zeros((rows, width), jnp.float32)
    out_im = jnp.zeros((rows, width), jnp.float32)
    for index in range(subgrids):
        re = back[index * rows : (index + 1) * rows, :width]
        im = back[index * rows : (index + 1) * rows, width:]
        c = mod_c[index : index + 1, :]
        s = mod_s[index : index + 1, :]
        out_re = out_re + (re * c - im * s)
        out_im = out_im + (re * s + im * c)
    weight = prolate_ref[...] * (1.0 / math.sqrt(subgrids * POINTS))
    image_ref[0] = out_re * weight
    image_ref[1] = out_im * weight


def gather(value, facets):
    together = value[None]
    distance = facets // 2
    while distance:
        pairs = [(index, index ^ distance) for index in range(facets)]
        together = jnp.concatenate([together, lax.ppermute(together, "facet", pairs)], 0)
        distance //= 2
    return together


VMEM = pl.BlockSpec(memory_space=pltpu.VMEM)
SMEM = pl.BlockSpec(memory_space=pltpu.SMEM)


def call(kernel, inputs, outputs, scratch, name):
    return pl.pallas_call(
        kernel,
        in_specs=inputs,
        out_specs=jax.tree.map(lambda _: VMEM, outputs),
        out_shape=outputs,
        scratch_shapes=scratch,
        name=name,
        compiler_params=pltpu.CompilerParams(vmem_limit_bytes=40 << 20),
    )


def local(facets, sky_strips, prolate, subgrid_offset, owner, observed, vis_uv, vis_count):
    parts, rows, width = sky_strips.shape
    slots, _, _, total = observed.shape
    subgrids = owner.shape[0]
    modulus = width * facets
    shape = jax.ShapeDtypeStruct
    me = lax.axis_index("facet").astype(jnp.int32).reshape(1)
    weight = prolate.reshape(1, width)

    table, coarse, fine = call(
        functools.partial(prepare_kernel, modulus, slots),
        [VMEM],
        (
            shape((2 * width, 2 * POINTS), jnp.bfloat16),
            shape((slots, BLOCK, total), jnp.bfloat16),
            shape((slots, 2, rows, total), jnp.float32),
        ),
        [pltpu.VMEM((STEP, 2 * POINTS), jnp.float32)] * 2
        + [pltpu.VMEM((width // STEP, 2 * POINTS), jnp.float32)] * 2,
        "prepare",
    )(vis_uv)

    sky = gather(sky_strips, facets)
    residual, update = call(
        functools.partial(visibility_kernel, modulus, facets),
        [SMEM] * 4 + [VMEM] * 6,
        (
            shape((slots, 2, rows, total), jnp.bfloat16),
            shape((slots, rows, 2 * POINTS), jnp.bfloat16),
        ),
        [
            pltpu.VMEM((slots * facets * rows, 2 * width), jnp.bfloat16),
            pltpu.VMEM((slots * facets * rows, 2 * POINTS), jnp.float32),
        ]
        + [pltpu.VMEM((slots, facets, width), jnp.float32)] * 2
        + [pltpu.VMEM((facets, 2 * POINTS), jnp.float32)] * 2,
        "visibility",
    )(me, owner, subgrid_offset, vis_count, sky, weight, table, coarse, fine, observed)

    updates = gather(update, facets).reshape(facets * slots, rows, 2 * POINTS)
    image = call(
        functools.partial(image_kernel, modulus, facets, slots),
        [SMEM, SMEM] + [VMEM] * 4,
        shape((2, rows, width), jnp.float32),
        [pltpu.VMEM((subgrids * rows, 2 * POINTS), jnp.bfloat16)]
        + [pltpu.VMEM((subgrids, width), jnp.float32)] * 2
        + [pltpu.SMEM((facets,), jnp.int32), pltpu.SMEM((subgrids,), jnp.int32)],
        "image",
    )(me, owner, subgrid_offset.reshape(subgrids, 1), updates, weight, table)
    return residual, image


def solution(mesh):
    in_specs = (
        P(None, "groups", "facet"),
        P(),
        P(),
        P(),
        P(("groups", "facet"), None, None, None),
        P(("groups", "facet"), None),
        P(("groups", "facet")),
    )
    out_specs = (P(("groups", "facet"), None, None, None), P(None, "groups", "facet"))
    return jax.shard_map(
        functools.partial(local, mesh.shape["facet"]),
        mesh=mesh,
        in_specs=in_specs,
        out_specs=out_specs,
        check_vma=False,
    )
```

time: 344 us -> 69.6 us (0.20)
  other arithmetic: 183 us -> 2.37 us
  matrix products: 63.4 us -> 0 us
  local copies, waits for them, and re-layouts: 47.8 us -> 16.1 us
  blocking collectives: 21.3 us -> 0 us
  Pallas kernels: 0 us -> 19.8 us
  waiting for transfers between devices: 6.49 us -> 17.6 us
  loops' own time: 10.2 us -> 0 us
  starting transfers between devices: 7.55 us -> 12.3 us
    another operation x41 -> x0, other arithmetic: 153 us -> none
    dot_general x34 -> x0, matrix products: 63.4 us -> none  [local_product(): return jnp.dot(first, second, preferred_element_type=jnp.float32)]
    all_gather x1 -> x0, blocking collectives: 21.3 us -> none  [local(): lax.all_gather(updates, 'facet', axis=0, tiled=True)]
    dynamic_slice x33 -> x0, local copies, waits for them, and re-layouts: 20.7 us -> none  [the longest x32 20.6 us: degrid_slot(): lax.scan(degrid_visit, initial, (jnp.arange(blocks, dtype=jnp.int32), coo...]
    and x17 -> x0, other arithmetic: 20.3 us -> none  [the longest x16 20.3 us: degrid_visit(): live = (position * block + within < live_count) & is_held]
    pallas_call x0 -> x3, Pallas kernels: none -> 19.8 us  [the longest x1 11.5 us: local(): call(functools.partial(visibility_kernel, modulus, facets), [SMEM] * 4 +...]
    slice x23 -> x0, local copies, waits for them, and re-layouts: 19.7 us -> none  [the longest x16 17.3 us: degrid_visit(): obs_block[0] - model[:, :block]]
    ppermute x0 -> x8, waiting for transfers between devices: none -> 17.6 us  [gather(): lax.ppermute(together, 'facet', pairs)]
  transfers between devices with their start and end apart: 1 -> 8, of which waited for: 1 -> 7; matrix products, arithmetic and copies ran while one was open for 2% -> 1% of each run, Pallas kernels for 0% -> 6%
where the time goes in v1:
time: 69.6 us; the launch traced here: 69 us
  Pallas kernels  19.8 us (28%)
  waiting for transfers between devices  17.6 us (25%)
  local copies, waits for them, and re-layouts  16.1 us (23%)
  starting transfers between devices  12.3 us (18%)
  other arithmetic  2.37 us (3%)
  between operations  0.79 us (1%)
    ppermute x8, waiting for transfers between devices, gather(): lax.ppermute(together, 'facet', pairs)  17.6 us
    unnamed x36, local copies, waits for them, and re-layouts  16 us
    ppermute x8, starting transfers between devices, gather(): lax.ppermute(together, 'facet', pairs)  12.3 us
    pallas_call x1, Pallas kernels, local(): call(functools.partial(visibility_kernel, modulus, facets), [SMEM] * 4 +...  11.5 us
    pallas_call x1, Pallas kernels, local(): call(functools.partial(prepare_kernel, modulus, slots), [VMEM], (shape((2...  4.48 us
    pallas_call x1, Pallas kernels, local(): call(functools.partial(image_kernel, modulus, facets, slots), [SMEM, SMEM...  3.86 us
    concatenate x6, other arithmetic, gather(): jnp.concatenate([together, lax.ppermute(together, 'facet', pairs)], 0)  2.37 us
  transfers between devices with their start and end apart: 8, of which 7 were waited for; matrix products, arithmetic and copies ran while one was open for 1% of the time, Pallas kernels for 6%

profile of v1, /device:TPU:0, one launch (start us, length us, event | category | flops | bytes accessed | tf_op | source)
XLA Modules:
  0.0 69.0 jit_solution(8014344681773960569)
XLA Ops:
  0.6 4.1 %collective-permute-start = (bf16[1,2,8,1024]{3,2,1,0:T(8,128)(2,1)}, bf16[1,2,8,1024]{3,2,1,0:T(8,128)(2,1)S(1)}, u32[]{:S(2)}, u32[]{:S(2)}) collective-permute-start(bf16[1,2,8,1024]{3,2,1,0:T(8,128)(2,1)} %bitcast.16), channel_id=1, source_target_pairs={{0,8},{1,9},{2,10},{3,11},{4,12},{5,13},{6,14},{7,15},{8,0},{9,1},... | collective-permute-start | bytes 98312 | tf_op jit(solution)/shard_map/ppermute | solution.py:348
  4.8 2.5 %collective-permute-done = bf16[1,2,8,1024]{3,2,1,0:T(8,128)(2,1)S(1)} collective-permute-done((bf16[1,2,8,1024]{3,2,1,0:T(8,128)(2,1)}, bf16[1,2,8,1024]{3,2,1,0:T(8,128)(2,1)S(1)}, u32[]{:S(2)}, u32[]{:S(2)}) %collective-permute-start) | collective-permute-done | bytes 32800 | tf_op jit(solution)/shard_map/ppermute | solution.py:348
  7.2 0.8 %pad_maximum_fusion.4 = bf16[2,2,8,1024]{3,2,1,0:T(8,128)(2,1)S(1)} fusion(bf16[1,2,8,1024]{3,2,1,0:T(8,128)(2,1)S(1)} %collective-permute-done, bf16[1,2,8,1024]{3,2,1,0:T(8,128)(2,1)} %bitcast.17), kind=kLoop, calls=%fused_computation.4 | loop fusion | flops 32768 | bytes 131072 | tf_op jit(solution)/shard_map/concatenate | solution.py:348
  8.0 1.6 %collective-permute-start.1 = (bf16[2,2,8,1024]{3,2,1,0:T(8,128)(2,1)S(1)}, bf16[2,2,8,1024]{3,2,1,0:T(8,128)(2,1)S(1)}, u32[]{:S(2)}, u32[]{:S(2)}) collective-permute-start(bf16[2,2,8,1024]{3,2,1,0:T(8,128)(2,1)S(1)} %pad_maximum_fusion.4), channel_id=1, source_target_pairs={{0,4},{1,5},{2,6},{3,7},{4,0},{5,1},{6,2},{7,3},{8,12},{9,13},{10,... | collective-permute-start | bytes 196616 | tf_op jit(solution)/shard_map/ppermute | solution.py:348
  9.5 0.0 copy-start.6
  9.5 0.8 %copy-done.6 = f32[2,8192]{1,0:T(2,128)S(1)} copy-done((f32[2,8192]{1,0:T(2,128)S(1)}, f32[2,8192]{1,0:T(2,128)}, u32[]{:S(2)}) %copy-start.6) | copy-done | bytes 65560
  10.4 4.5 %prepare.1 = (bf16[2048,1024]{1,0:T(8,128)(2,1)S(1)}, bf16[2,128,8192]{2,1,0:T(8,128)(2,1)S(1)}, f32[2,2,8,8192]{3,2,1,0:T(8,128)S(1)}) custom-call(f32[2,8192]{1,0:T(2,128)S(1)} %copy-done.6), custom_call_target="tpu_custom_call" | custom-call | tf_op jit(solution)/shard_map/prepare/pallas_call | solution.py:378
  14.9 0.0 copy-start
  14.9 1.9 %copy-done = bf16[2048,1024]{1,0:T(8,128)(2,1)} copy-done((bf16[2048,1024]{1,0:T(8,128)(2,1)}, bf16[2048,1024]{1,0:T(8,128)(2,1)S(1)}, u32[]{:S(2)}) %copy-start) | copy-done | bytes 4194328
  16.8 0.0 copy-start.3
  16.8 2.0 %copy-done.3 = bf16[2,128,8192]{2,1,0:T(8,128)(2,1)} copy-done((bf16[2,128,8192]{2,1,0:T(8,128)(2,1)}, bf16[2,128,8192]{2,1,0:T(8,128)(2,1)S(1)}, u32[]{:S(2)}) %copy-start.3) | copy-done | bytes 4194328
  18.8 0.0 collective-permute-done.1
  18.8 0.8 %pad_maximum_fusion.2 = bf16[4,2,8,1024]{3,2,1,0:T(8,128)(2,1)S(1)} fusion(bf16[2,2,8,1024]{3,2,1,0:T(8,128)(2,1)S(1)} %collective-permute-done.1, bf16[1,2,8,1024]{3,2,1,0:T(8,128)(2,1)S(1)} %collective-permute-done, bf16[1,2,8,1024]{3,2,1,0:T(8,128)(2,1)} %bitcast.18), kind=kLoop, calls=%fused_computation.2 | loop fusion | flops 131072 | bytes 262144 | tf_op jit(solution)/shard_map/concatenate | solution.py:348
  19.6 1.6 %collective-permute-start.2 = (bf16[4,2,8,1024]{3,2,1,0:T(8,128)(2,1)S(1)}, bf16[4,2,8,1024]{3,2,1,0:T(8,128)(2,1)S(1)}, u32[]{:S(2)}, u32[]{:S(2)}) collective-permute-start(bf16[4,2,8,1024]{3,2,1,0:T(8,128)(2,1)S(1)} %pad_maximum_fusion.2), channel_id=1, source_target_pairs={{0,2},{1,3},{2,0},{3,1},{4,6},{5,7},{6,4},{7,5},{8,10},{9,11},{10,... | collective-permute-start | bytes 393224 | tf_op jit(solution)/shard_map/ppermute | solution.py:348
  21.2 0.8 %constant_dynamic-update-slice_fusion.4 = bf16[16,2,8,1024]{3,2,1,0:T(8,128)(2,1)S(1)} fusion(bf16[2,8,1024]{2,1,0:T(8,128)(2,1)} %param.7), kind=kLoop, calls=%fused_computation.10 | loop fusion | bytes 65536
  21.9 2.7 %collective-permute-done.2 = bf16[4,2,8,1024]{3,2,1,0:T(8,128)(2,1)S(1)} collective-permute-done((bf16[4,2,8,1024]{3,2,1,0:T(8,128)(2,1)S(1)}, bf16[4,2,8,1024]{3,2,1,0:T(8,128)(2,1)S(1)}, u32[]{:S(2)}, u32[]{:S(2)}) %collective-permute-start.2) | collective-permute-done | bytes 131104 | tf_op jit(solution)/shard_map/ppermute | solution.py:348
  24.6 0.8 %pad_maximum_fusion = bf16[8,2,8,1024]{3,2,1,0:T(8,128)(2,1)S(1)} fusion(bf16[4,2,8,1024]{3,2,1,0:T(8,128)(2,1)S(1)} %collective-permute-done.2, bf16[2,2,8,1024]{3,2,1,0:T(8,128)(2,1)S(1)} %collective-permute-done.1, bf16[1,2,8,1024]{3,2,1,0:T(8,128)(2,1)S(1)} %collective-permute-done, bf16[1,2,8,1024]{3,2,1,0:T(8,128)(2,1)} %bitcast.19), kind=kLoop, calls=%fused_computation | loop fusion | flops 393216 | bytes 524288 | tf_op jit(solution)/shard_map/concatenate | solution.py:348
  25.4 0.1 collective-permute-start.3
  25.5 1.5 %collective-permute-done.3 = bf16[8,2,8,1024]{3,2,1,0:T(8,128)(2,1)S(1)} collective-permute-done((bf16[8,2,8,1024]{3,2,1,0:T(8,128)(2,1)S(1)}, bf16[8,2,8,1024]{3,2,1,0:T(8,128)(2,1)S(1)}, u32[]{:S(2)}, u32[]{:S(2)}) %collective-permute-start.3) | collective-permute-done | bytes 262176 | tf_op jit(solution)/shard_map/ppermute | solution.py:348
  27.0 0.0 copy-start.1
  27.0 2.2 %copy-done.1 = bf16[2048,1024]{1,0:T(8,128)(2,1)S(1)} copy-done((bf16[2048,1024]{1,0:T(8,128)(2,1)S(1)}, bf16[2048,1024]{1,0:T(8,128)(2,1)}, u32[]{:S(2)}) %copy-start.1) | copy-done | bytes 4194328
  29.2 0.0 copy-start.4
  29.2 2.2 %copy-done.4 = bf16[2,128,8192]{2,1,0:T(8,128)(2,1)S(1)} copy-done((bf16[2,128,8192]{2,1,0:T(8,128)(2,1)S(1)}, bf16[2,128,8192]{2,1,0:T(8,128)(2,1)}, u32[]{:S(2)}) %copy-start.4) | copy-done | bytes 4194328
  31.4 0.0 copy-start.5
  31.4 1.2 %copy-done.5 = f32[2,2,8,8192]{3,2,1,0:T(8,128)S(1)} copy-done((f32[2,2,8,8192]{3,2,1,0:T(8,128)S(1)}, f32[2,2,8,8192]{3,2,1,0:T(8,128)}, u32[]{:S(2)}) %copy-start.5) | copy-done | bytes 1048600
  32.6 0.0 copy-start.7
  32.6 0.7 copy-done.7
  33.3 0.0 copy-start.9
  33.3 0.7 copy-done.9
  34.0 0.0 copy-start.11
  34.0 0.7 copy-done.11
  34.6 0.0 copy-start.13
  34.6 0.7 copy-done.13
  35.3 0.0 copy-start.12
  35.3 0.0 copy-start.8
  35.3 0.0 copy-start.10
  35.3 11.5 %visibility.1 = (bf16[2,2,8,8192]{3,2,1,0:T(8,128)(2,1)}, bf16[2,8,1024]{2,1,0:T(8,128)(2,1)S(1)}) custom-call(s32[1]{0:T(128)} %bitcast.me_ref, s32[16]{0:T(128)S(1)} %copy-done.9, s32[16]{0:T(128)S(1)} %copy-done.11, s32[2]{0:T(128)S(1)} %copy-done.13, bf16[16,2,8,1024]{3,2,1,0:T(8,128)(2,1)S(1)} %constant_dynamic-update-slice_fusion.sky_ref, ...), custom_call_target="tpu_custom_call" | custom-call | tf_op jit(solution)/shard_map/visibility/pallas_call | solution.py:392
  46.8 2.8 %collective-permute-start.4 = (bf16[1,2,8,1024]{3,2,1,0:T(8,128)(2,1)S(1)}, bf16[1,2,8,1024]{3,2,1,0:T(8,128)(2,1)S(1)}, u32[]{:S(2)}, u32[]{:S(2)}) collective-permute-start(bf16[1,2,8,1024]{3,2,1,0:T(8,128)(2,1)S(1)} %bitcast.9), channel_id=1, source_target_pairs={{0,8},{1,9},{2,10},{3,11},{4,12},{5,13},{6,14},{7,15},{8,0},{9,1},... | collective-permute-start | bytes 98312 | tf_op jit(solution)/shard_map/ppermute | solution.py:348
  49.6 2.2 %collective-permute-done.4 = bf16[1,2,8,1024]{3,2,1,0:T(8,128)(2,1)S(1)} collective-permute-done((bf16[1,2,8,1024]{3,2,1,0:T(8,128)(2,1)S(1)}, bf16[1,2,8,1024]{3,2,1,0:T(8,128)(2,1)S(1)}, u32[]{:S(2)}, u32[]{:S(2)}) %collective-permute-start.4) | collective-permute-done | bytes 32800 | tf_op jit(solution)/shard_map/ppermute | solution.py:348
  51.9 0.3 collective-permute-start.5
  52.2 0.0 copy-done.12
  52.2 0.1 copy.9.offset_ref
  52.3 3.9 %collective-permute-done.5 = bf16[2,2,8,1024]{3,2,1,0:T(8,128)(2,1)S(1)} collective-permute-done((bf16[2,2,8,1024]{3,2,1,0:T(8,128)(2,1)S(1)}, bf16[2,2,8,1024]{3,2,1,0:T(8,128)(2,1)S(1)}, u32[]{:S(2)}, u32[]{:S(2)}) %collective-permute-start.5) | collective-permute-done | bytes 65568 | tf_op jit(solution)/shard_map/ppermute | solution.py:348
  56.2 1.7 %collective-permute-start.6 = (bf16[4,2,8,1024]{3,2,1,0:T(8,128)(2,1)S(1)}, bf16[4,2,8,1024]{3,2,1,0:T(8,128)(2,1)S(1)}, u32[]{:S(2)}, u32[]{:S(2)}) collective-permute-start(bf16[4,2,8,1024]{3,2,1,0:T(8,128)(2,1)S(1)} %pad_maximum_fusion.3), channel_id=1, source_target_pairs={{0,2},{1,3},{2,0},{3,1},{4,6},{5,7},{6,4},{7,5},{8,10},{9,11},{10,... | collective-permute-start | bytes 393224 | tf_op jit(solution)/shard_map/ppermute | solution.py:348
  57.9 3.3 %collective-permute-done.6 = bf16[4,2,8,1024]{3,2,1,0:T(8,128)(2,1)S(1)} collective-permute-done((bf16[4,2,8,1024]{3,2,1,0:T(8,128)(2,1)S(1)}, bf16[4,2,8,1024]{3,2,1,0:T(8,128)(2,1)S(1)}, u32[]{:S(2)}, u32[]{:S(2)}) %collective-permute-start.6) | collective-permute-done | bytes 131104 | tf_op jit(solution)/shard_map/ppermute | solution.py:348
  61.3 0.1 collective-permute-start.7
  61.4 1.5 %collective-permute-done.7 = bf16[8,2,8,1024]{3,2,1,0:T(8,128)(2,1)S(1)} collective-permute-done((bf16[8,2,8,1024]{3,2,1,0:T(8,128)(2,1)S(1)}, bf16[8,2,8,1024]{3,2,1,0:T(8,128)(2,1)S(1)}, u32[]{:S(2)}, u32[]{:S(2)}) %collective-permute-start.7) | collective-permute-done | bytes 262176 | tf_op jit(solution)/shard_map/ppermute | solution.py:348
  62.9 0.0 copy-done.8
  62.9 0.0 copy-done.10
  62.9 0.0 copy-start.2
  62.9 2.2 %copy-done.2 = bf16[2048,1024]{1,0:T(8,128)(2,1)S(1)} copy-done((bf16[2048,1024]{1,0:T(8,128)(2,1)S(1)}, bf16[2048,1024]{1,0:T(8,128)(2,1)}, u32[]{:S(2)}) %copy-start.2) | copy-done | bytes 4194328
  65.1 3.9 %image.1 = f32[2,8,1024]{2,1,0:T(8,128)} custom-call(s32[1]{0:T(128)} %bitcast.me_ref, s32[16]{0:T(128)S(1)} %copy-done.10, s32[16,1]{1,0:T(8,128)S(1)} %copy.9.offset_ref, bf16[32,8,1024]{2,1,0:T(8,128)(2,1)S(1)} %bitcast.8, f32[1,1024]{1,0:T(1,128)S(1)} %bitcast.14, bf16[2048,1024]{1,0:T(8,128)(2,1)S(1)} %copy-done.2), custom_call_target="tpu_custom_call" | custom-call | tf_op jit(solution)/shard_map/image/pallas_call | solution.py:409
  (12 shorter events, 0.1 us)
Async XLA Ops:
  0.6 6.6 %collective-permute-start = (bf16[1,2,8,1024]{3,2,1,0:T(8,128)(2,1)}, bf16[1,2,8,1024]{3,2,1,0:T(8,128)(2,1)S(1)}, u32[]{:S(2)}, u32[]{:S(2)}) collective-permute-start(bf16[1,2,8,1024]{3,2,1,0:T(8,128)(2,1)} %bitcast.16), channel_id=1, source_target_pairs={{0,8},{1,9},{2,10},{3,11},{4,12},{5,13},{6,14},{7,15},{8,0},{9,1},... | collective-permute-start | bytes 98312 | tf_op jit(solution)/shard_map/ppermute | solution.py:348
  8.0 10.8 %collective-permute-start.1 = (bf16[2,2,8,1024]{3,2,1,0:T(8,128)(2,1)S(1)}, bf16[2,2,8,1024]{3,2,1,0:T(8,128)(2,1)S(1)}, u32[]{:S(2)}, u32[]{:S(2)}) collective-permute-start(bf16[2,2,8,1024]{3,2,1,0:T(8,128)(2,1)S(1)} %pad_maximum_fusion.4), channel_id=1, source_target_pairs={{0,4},{1,5},{2,6},{3,7},{4,0},{5,1},{6,2},{7,3},{8,12},{9,13},{10,... | collective-permute-start | bytes 196616 | tf_op jit(solution)/shard_map/ppermute | solution.py:348
  9.5 0.8 %copy-start.6 = (f32[2,8192]{1,0:T(2,128)S(1)}, f32[2,8192]{1,0:T(2,128)}, u32[]{:S(2)}) copy-start(f32[2,8192]{1,0:T(2,128)} %uv_ref.1) | copy-start | bytes 196612
  14.9 1.9 %copy-start = (bf16[2048,1024]{1,0:T(8,128)(2,1)}, bf16[2048,1024]{1,0:T(8,128)(2,1)S(1)}, u32[]{:S(2)}) copy-start(bf16[2048,1024]{1,0:T(8,128)(2,1)S(1)} %get-tuple-element.7.table_ref) | copy-start | bytes 12582916
  16.8 2.0 %copy-start.3 = (bf16[2,128,8192]{2,1,0:T(8,128)(2,1)}, bf16[2,128,8192]{2,1,0:T(8,128)(2,1)S(1)}, u32[]{:S(2)}) copy-start(bf16[2,128,8192]{2,1,0:T(8,128)(2,1)S(1)} %get-tuple-element.8.coarse_ref) | copy-start | bytes 12582916
  19.6 5.0 %collective-permute-start.2 = (bf16[4,2,8,1024]{3,2,1,0:T(8,128)(2,1)S(1)}, bf16[4,2,8,1024]{3,2,1,0:T(8,128)(2,1)S(1)}, u32[]{:S(2)}, u32[]{:S(2)}) collective-permute-start(bf16[4,2,8,1024]{3,2,1,0:T(8,128)(2,1)S(1)} %pad_maximum_fusion.2), channel_id=1, source_target_pairs={{0,2},{1,3},{2,0},{3,1},{4,6},{5,7},{6,4},{7,5},{8,10},{9,11},{10,... | collective-permute-start | bytes 393224 | tf_op jit(solution)/shard_map/ppermute | solution.py:348
  25.4 1.6 %collective-permute-start.3 = (bf16[8,2,8,1024]{3,2,1,0:T(8,128)(2,1)S(1)}, bf16[8,2,8,1024]{3,2,1,0:T(8,128)(2,1)S(1)}, u32[]{:S(2)}, u32[]{:S(2)}) collective-permute-start(bf16[8,2,8,1024]{3,2,1,0:T(8,128)(2,1)S(1)} %pad_maximum_fusion), channel_id=1, source_target_pairs={{0,1},{1,0},{2,3},{3,2},{4,5},{5,4},{6,7},{7,6},{8,9},{9,8},{10,11... | collective-permute-start | bytes 786440 | tf_op jit(solution)/shard_map/ppermute | solution.py:348
  27.0 2.2 %copy-start.1 = (bf16[2048,1024]{1,0:T(8,128)(2,1)S(1)}, bf16[2048,1024]{1,0:T(8,128)(2,1)}, u32[]{:S(2)}) copy-start(bf16[2048,1024]{1,0:T(8,128)(2,1)} %copy-done) | copy-start | bytes 12582916
  29.2 2.2 %copy-start.4 = (bf16[2,128,8192]{2,1,0:T(8,128)(2,1)S(1)}, bf16[2,128,8192]{2,1,0:T(8,128)(2,1)}, u32[]{:S(2)}) copy-start(bf16[2,128,8192]{2,1,0:T(8,128)(2,1)} %copy-done.3) | copy-start | bytes 12582916
  31.4 1.2 %copy-start.5 = (f32[2,2,8,8192]{3,2,1,0:T(8,128)S(1)}, f32[2,2,8,8192]{3,2,1,0:T(8,128)}, u32[]{:S(2)}) copy-start(f32[2,2,8,8192]{3,2,1,0:T(8,128)} %observed_ref.1) | copy-start | bytes 3145732
  32.6 0.7 copy-start.7
  33.3 0.7 copy-start.9
  34.0 0.7 copy-start.11
  34.6 0.7 copy-start.13
  35.3 16.9 %copy-start.12 = (s32[16]{0:T(128)S(1)}, s32[16]{0:T(128)}, u32[]{:S(2)}) copy-start(s32[16]{0:T(128)} %offset_ref.1) | copy-start | bytes 196
  35.3 27.6 %copy-start.8 = (f32[1024]{0:T(1024)S(1)}, f32[1024]{0:T(1024)}, u32[]{:S(2)}) copy-start(f32[1024]{0:T(1024)} %param.8) | copy-start | bytes 12292
  35.3 27.6 %copy-start.10 = (s32[16]{0:T(128)S(1)}, s32[16]{0:T(128)}, u32[]{:S(2)}) copy-start(s32[16]{0:T(128)} %owner_ref.3) | copy-start | bytes 196
  46.8 5.1 %collective-permute-start.4 = (bf16[1,2,8,1024]{3,2,1,0:T(8,128)(2,1)S(1)}, bf16[1,2,8,1024]{3,2,1,0:T(8,128)(2,1)S(1)}, u32[]{:S(2)}, u32[]{:S(2)}) collective-permute-start(bf16[1,2,8,1024]{3,2,1,0:T(8,128)(2,1)S(1)} %bitcast.9), channel_id=1, source_target_pairs={{0,8},{1,9},{2,10},{3,11},{4,12},{5,13},{6,14},{7,15},{8,0},{9,1},... | collective-permute-start | bytes 98312 | tf_op jit(solution)/shard_map/ppermute | solution.py:348
  51.9 4.3 %collective-permute-start.5 = (bf16[2,2,8,1024]{3,2,1,0:T(8,128)(2,1)S(1)}, bf16[2,2,8,1024]{3,2,1,0:T(8,128)(2,1)S(1)}, u32[]{:S(2)}, u32[]{:S(2)}) collective-permute-start(bf16[2,2,8,1024]{3,2,1,0:T(8,128)(2,1)S(1)} %pad_maximum_fusion.5), channel_id=1, source_target_pairs={{0,4},{1,5},{2,6},{3,7},{4,0},{5,1},{6,2},{7,3},{8,12},{9,13},{10,... | collective-permute-start | bytes 196616 | tf_op jit(solution)/shard_map/ppermute | solution.py:348
  56.2 5.0 %collective-permute-start.6 = (bf16[4,2,8,1024]{3,2,1,0:T(8,128)(2,1)S(1)}, bf16[4,2,8,1024]{3,2,1,0:T(8,128)(2,1)S(1)}, u32[]{:S(2)}, u32[]{:S(2)}) collective-permute-start(bf16[4,2,8,1024]{3,2,1,0:T(8,128)(2,1)S(1)} %pad_maximum_fusion.3), channel_id=1, source_target_pairs={{0,2},{1,3},{2,0},{3,1},{4,6},{5,7},{6,4},{7,5},{8,10},{9,11},{10,... | collective-permute-start | bytes 393224 | tf_op jit(solution)/shard_map/ppermute | solution.py:348
  61.3 1.6 %collective-permute-start.7 = (bf16[8,2,8,1024]{3,2,1,0:T(8,128)(2,1)S(1)}, bf16[8,2,8,1024]{3,2,1,0:T(8,128)(2,1)S(1)}, u32[]{:S(2)}, u32[]{:S(2)}) collective-permute-start(bf16[8,2,8,1024]{3,2,1,0:T(8,128)(2,1)S(1)} %pad_maximum_fusion.1), channel_id=1, source_target_pairs={{0,1},{1,0},{2,3},{3,2},{4,5},{5,4},{6,7},{7,6},{8,9},{9,8},{10,11... | collective-permute-start | bytes 786440 | tf_op jit(solution)/shard_map/ppermute | solution.py:348
  62.9 2.2 %copy-start.2 = (bf16[2048,1024]{1,0:T(8,128)(2,1)S(1)}, bf16[2048,1024]{1,0:T(8,128)(2,1)}, u32[]{:S(2)}) copy-start(bf16[2048,1024]{1,0:T(8,128)(2,1)} %copy-done) | copy-start | bytes 12582916

commit v2 on v1

v2 whole, which is shorter than its diff:
```python
import functools
import math

import jax
import jax.numpy as jnp
from jax import lax
from jax.experimental import pallas as pl
from jax.experimental.pallas import tpu as pltpu
from jax.sharding import PartitionSpec as P


POINTS = 512
FINE = 8
COARSE = POINTS // FINE
BLOCK = 2 * COARSE
ROOT = 8
STEP = 64
FAR = 4
CHUNK = 512

COS = (
    0.9999999890590217, -4.934801124863452, 4.058694841243232, -1.3351584301691248,
    0.23502980840046309, -0.025358983639642813, 0.001593910683444594,
)
SIN = (
    3.14159265125575, -5.167712550664621, 2.550160355805489, -0.5992423074495862,
    0.08208188864038139, -0.00727531575291481, 0.00039528045693413335,
)


def horner(coefficients, z):
    total = coefficients[-1] * z + coefficients[-2]
    for value in coefficients[-3::-1]:
        total = total * z + value
    return total


def turn(t):
    y = 2.0 * (t - jnp.floor(t + 0.5))
    z = y * y
    return horner(COS, z), horner(SIN, z) * y


def modular(first, second, modulus):
    if modulus & (modulus - 1) == 0:
        return (first * second) & (modulus - 1)
    upper = second // 256
    lower = second % 256
    return (first * lower % modulus + first * upper % modulus * 256 % modulus) % modulus


def iota(shape, axis):
    return lax.broadcasted_iota(jnp.int32, shape, axis)


def column_points(shape):
    column = iota(shape, 1)
    return (column % COARSE) * FINE + column // BLOCK, (column // COARSE) % 2


def facet_at(position, me, facets):
    far = min(FAR, facets)
    near = facets // far
    bits = near.bit_length() - 1
    flipped = me & (near - 1)
    for bit in range(bits):
        flipped = flipped ^ (((position // far >> bit) & 1) << (bits - 1 - bit))
    return (me // near - position % far + far) % far * near + flipped


def position_of(facet, me, facets):
    far = min(FAR, facets)
    near = facets // far
    bits = near.bit_length() - 1
    flipped = 0
    for bit in range(bits):
        flipped = flipped | ((((facet ^ me) >> bit) & 1) << (bits - 1 - bit))
    return (me // near - facet // near + far) % far + far * flipped


def swap(block):
    return pltpu.roll(block, COARSE, 1)


def blocks_of(value):
    return [value[:, b * BLOCK : (b + 1) * BLOCK] for b in range(FINE)]


def find_offsets(me, owner_ref, offset_ref, slots):
    def find(index, carry):
        held, offsets = carry
        mine = owner_ref[index] == me
        offsets = tuple(
            jnp.where(mine & (held == slot), offset_ref[index], offsets[slot]) for slot in range(slots)
        )
        return held + mine.astype(jnp.int32), offsets

    zero = jnp.int32(0)
    return lax.fori_loop(0, owner_ref.shape[0], find, (zero, (zero,) * slots))


def fraction_of(first, second, modulus):
    return modular(first, second, modulus).astype(jnp.float32) * (1.0 / modulus)


def fetch(copies, semaphores):
    started = [
        pltpu.make_async_copy(source, target, semaphores.at[index])
        for index, (source, target) in enumerate(copies)
    ]
    for copy in started:
        copy.start()
    for copy in started:
        copy.wait()


def setup_kernel(
    modulus,
    slots,
    sky_hbm,
    owner_hbm,
    offset_hbm,
    count_hbm,
    prolate_hbm,
    sky_ref,
    mod_ref,
    turn_ref,
    live_ref,
    owner_ref,
    offset_ref,
    count_ref,
    prolate_ref,
    semaphores,
):
    fetch(
        (
            (sky_hbm, sky_ref),
            (owner_hbm, owner_ref),
            (offset_hbm, offset_ref),
            (count_hbm, count_ref),
            (prolate_hbm, prolate_ref),
        ),
        semaphores,
    )
    me = lax.axis_index("facet")
    facets, width = mod_ref.shape[2:]
    held, offsets = find_offsets(me, owner_ref, offset_ref, slots)
    weight = prolate_ref[...]

    facet = facet_at(iota((facets, width), 0), me, facets)
    across = facet * width + iota((facets, width), 1)
    for slot in range(slots):
        c, s = turn(fraction_of(across, offsets[slot], modulus))
        mod_ref[0, slot] = c * weight
        mod_ref[1, slot] = s * weight
        live_ref[slot] = jnp.full(live_ref.shape[1:], jnp.where(slot < held, count_ref[slot], 0))

    points, part = column_points((facets, 2 * POINTS))
    facet = facet_at(iota(points.shape, 0), me, facets)
    c, s = turn(fraction_of(facet, points, facets))
    scale = 1.0 / math.sqrt(modulus)
    turn_ref[0] = c * scale
    turn_ref[1] = jnp.where(part == 0, -s, s) * scale


def plan_kernel(
    modulus,
    owner_hbm,
    offset_hbm,
    prolate_hbm,
    residual_ref,
    back_ref,
    lift_ref,
    residual_hbm,
    owner_ref,
    offset_ref,
    prolate_ref,
    semaphores,
):
    leaving = pltpu.make_async_copy(residual_ref, residual_hbm, semaphores.at[3])
    leaving.start()
    fetch(
        ((owner_hbm, owner_ref), (offset_hbm, offset_ref), (prolate_hbm, prolate_ref)), semaphores
    )
    me = lax.axis_index("facet")
    facets = lax.axis_size("facet")
    subgrids, width = back_ref.shape[1:]
    row = iota((subgrids, 128), 0)

    def place_offset(index, placed):
        return jnp.where(row == index, offset_ref[index], placed)

    column = lax.fori_loop(0, subgrids, place_offset, jnp.zeros(row.shape, jnp.int32), unroll=True)
    across = me * width + iota((subgrids, width), 1)
    c, s = turn(fraction_of(across, jnp.concatenate([column] * (width // 128), 1), modulus))
    weight = prolate_ref[...] * (1.0 / math.sqrt(subgrids * POINTS))
    back_ref[0] = c * weight
    back_ref[1] = s * weight

    points, part = column_points(lift_ref.shape[1:])
    c, s = turn(fraction_of(me, points, facets))
    lift_ref[0] = c
    lift_ref[1] = jnp.where(part == 0, -s, s)
    leaving.wait()


def table_kernel(modulus, table_ref, v_re, v_im, u_re, u_im):
    width = table_ref.shape[0] // 2
    points, part = column_points(v_re.shape)
    fraction = fraction_of(iota(v_re.shape, 0), points, modulus)
    v_re[...], v_im[...] = turn(fraction + 0.25 * part.astype(jnp.float32))
    points, _ = column_points(u_re.shape)
    u_re[...], u_im[...] = turn(fraction_of(iota(u_re.shape, 0) * STEP, points, modulus))

    def table_step(step, _):
        c = u_re[pl.ds(step, 1), :]
        s = u_im[pl.ds(step, 1), :]
        row = pl.multiple_of(step * STEP, STEP)
        table_ref[pl.ds(row, STEP), :] = (v_re[...] * c - v_im[...] * s).astype(jnp.bfloat16)
        table_ref[pl.ds(width + row, STEP), :] = (v_re[...] * s + v_im[...] * c).astype(jnp.bfloat16)
        return 0

    lax.fori_loop(0, width // STEP, table_step, 0)


def back_table_kernel(modulus, table_ref, v_re, v_im, u_re, u_im):
    width = table_ref.shape[1] // 2
    row = iota(v_re.shape, 0)
    fraction = fraction_of(iota(v_re.shape, 1), row % COARSE * FINE, modulus)
    v_re[...], v_im[...] = turn(fraction + 0.25 * (row // COARSE).astype(jnp.float32))
    u_re[...], u_im[...] = turn(fraction_of(iota(u_re.shape, 1), iota(u_re.shape, 0), modulus))

    def table_step(b, _):
        c = u_re[pl.ds(b, 1), :]
        s = u_im[pl.ds(b, 1), :]
        at = pl.ds(pl.multiple_of(b * BLOCK, BLOCK), BLOCK)
        table_ref[at, :width] = (v_re[...] * c - v_im[...] * s).astype(jnp.bfloat16)
        table_ref[at, width:] = (v_re[...] * s + v_im[...] * c).astype(jnp.bfloat16)
        return 0

    lax.fori_loop(0, FINE, table_step, 0)


def coarse_kernel(slot, uv_ref, coarse_ref, fine_ref):
    total = uv_ref.shape[1]
    chunk = min(512, total)

    def coarse_step(step, _):
        at = pl.ds(pl.multiple_of(step * chunk, chunk), chunk)
        u = jnp.broadcast_to(uv_ref[slot : slot + 1, at], (ROOT, chunk))
        fine = u * (1.0 / POINTS)
        fine_ref[0, :, at], fine_ref[1, :, at] = turn(fine)
        low = u * (FINE / POINTS)
        low = low - jnp.floor(low)
        re, im = turn(low * iota(u.shape, 0).astype(jnp.float32))
        c, s = turn(u * (FINE * ROOT / POINTS))
        for pair in range(ROOT // 2):
            next_re = re * c - im * s
            next_im = re * s + im * c
            rows = pair * 2 * ROOT
            coarse_ref[rows : rows + 2 * ROOT, at] = jnp.concatenate(
                [re, next_re], 0
            ).astype(jnp.bfloat16)
            coarse_ref[COARSE + rows : COARSE + rows + 2 * ROOT, at] = jnp.concatenate(
                [im, next_im], 0
            ).astype(jnp.bfloat16)
            re = next_re * c - next_im * s
            im = next_re * s + next_im * c
        return 0

    lax.fori_loop(0, total // chunk, coarse_step, 0)


def grid_kernel(facets, sky_ref, mod_ref, turn_ref, table_ref, points_ref, lhs, raw):
    slots = mod_ref.shape[1]
    rows = sky_ref.shape[2]
    width = sky_ref.shape[3]

    for slot in range(slots):

        def modulate(pair, _):
            parts = []
            for which in range(2):
                position = pair * 2 + which
                c = mod_ref[0, slot, pl.ds(position, 1), :]
                s = mod_ref[1, slot, pl.ds(position, 1), :]
                re = sky_ref[position, 0].astype(jnp.float32)
                im = sky_ref[position, 1].astype(jnp.float32)
                parts.append((re * c + im * s, im * c - re * s))
            row = pl.multiple_of((slot * facets + pair * 2) * rows, 2 * rows)
            at = pl.ds(row, 2 * rows)
            lhs[at, :width] = jnp.concatenate([parts[0][0], parts[1][0]], 0).astype(jnp.bfloat16)
            lhs[at, width:] = jnp.concatenate([parts[0][1], parts[1][1]], 0).astype(jnp.bfloat16)
            return 0

        lax.fori_loop(0, facets // 2, modulate, 0, unroll=True)

    raw[...] = jnp.dot(lhs[...], table_ref[...], preferred_element_type=jnp.float32)
    first_half = jnp.where(iota((rows, BLOCK), 1) < COARSE, jnp.float32(1.0), jnp.float32(-1.0))

    for slot in range(slots):

        def add_facet(position, carry):
            straight, crossed = carry
            row = pl.multiple_of((slot * facets + position) * rows, rows)
            value = raw[pl.ds(row, rows), :]
            return (
                straight + value * turn_ref[0, pl.ds(position, 1), :],
                crossed + value * turn_ref[1, pl.ds(position, 1), :],
            )

        empty = jnp.zeros((rows, FINE * BLOCK), jnp.float32)
        straight, crossed = lax.fori_loop(0, facets, add_facet, (empty, empty), unroll=True)
        grid = [
            (first + swap(second)).astype(jnp.bfloat16).astype(jnp.float32)
            for first, second in zip(blocks_of(straight), blocks_of(crossed))
        ]
        points_ref[slot] = jnp.concatenate(
            [block * first_half for block in grid] + [swap(block) for block in grid], 0
        ).astype(jnp.bfloat16)


def visibility_kernel(slots, points_ref, live_ref, observed_ref, *refs):
    coarse_refs, fine_refs = refs[:slots], refs[slots : 2 * slots]
    residual_ref, update_ref = refs[2 * slots :]
    _, _, rows, total = observed_ref.shape
    chunk = min(CHUNK, total)
    first_half = jnp.where(iota((rows, BLOCK), 1) < COARSE, jnp.float32(1.0), jnp.float32(-1.0))

    for slot in range(slots):
        points_lhs = points_ref[slot]
        live = jnp.concatenate([live_ref[slot]] * (chunk // live_ref.shape[2]), 1)

        def visit(step, carry):
            at = pl.ds(pl.multiple_of(step * chunk, chunk), chunk)
            coarse = coarse_refs[slot][:, at]
            c = fine_refs[slot][0, :, at]
            s = fine_refs[slot][1, :, at]
            terms = jnp.dot(points_lhs, coarse, preferred_element_type=jnp.float32)
            half = FINE * rows
            re = terms[half - rows : half]
            im = terms[2 * half - rows :]
            for b in range(FINE - 2, -1, -1):
                re, im = (
                    terms[b * rows : (b + 1) * rows] + (re * c - im * s),
                    terms[half + b * rows : half + (b + 1) * rows] + (re * s + im * c),
                )
            scale = 1.0 / math.sqrt(POINTS)
            alive = step * chunk + iota((rows, chunk), 1) < live
            re = jnp.where(alive, observed_ref[slot, 0, :, at] - re * scale, 0.0).astype(jnp.bfloat16)
            im = jnp.where(alive, observed_ref[slot, 1, :, at] - im * scale, 0.0).astype(jnp.bfloat16)
            residual_ref[slot, 0, :, at] = re
            residual_ref[slot, 1, :, at] = im
            re = re.astype(jnp.float32)
            im = im.astype(jnp.float32)
            all_re, all_im = [re], [im]
            for _ in range(1, FINE):
                re, im = re * c + im * s, im * c - re * s
                all_re.append(re)
                all_im.append(im)
            spread = jnp.concatenate(all_re + all_im, 0).astype(jnp.bfloat16)
            return carry + lax.dot_general(
                spread, coarse, (((1,), (1,)), ((), ())), preferred_element_type=jnp.float32
            )

        gathered = lax.fori_loop(
            0, total // chunk, visit, jnp.zeros((2 * FINE * rows, BLOCK), jnp.float32), unroll=True
        )
        scale = 1.0 / math.sqrt(total)
        for b in range(FINE):
            re = gathered[b * rows : (b + 1) * rows]
            im = gathered[(FINE + b) * rows : (FINE + b + 1) * rows]
            update_ref[slot, :, b * BLOCK : (b + 1) * BLOCK] = (
                (swap(im) + re * first_half) * scale
            ).astype(jnp.bfloat16)


def image_kernel(
    facets,
    slots,
    owner_ref,
    update_ref,
    back_ref,
    lift_ref,
    table_ref,
    image_ref,
    lhs,
    taken,
    place,
):
    me = lax.axis_index("facet")
    subgrids = owner_ref.shape[0]
    rows = update_ref.shape[1]
    width = image_ref.shape[2]

    def clear(index, _):
        taken[index] = 0
        return 0

    lax.fori_loop(0, facets, clear, 0, unroll=True)

    def assign(index, _):
        holder = owner_ref[index]
        rank = taken[holder]
        taken[holder] = rank + 1
        place[index] = position_of(holder, me, facets) * slots + rank
        return 0

    lax.fori_loop(0, subgrids, assign, 0, unroll=True)

    straight = lift_ref[0]
    crossed = lift_ref[1]

    def lift(pair, _):
        parts = []
        for which in range(2):
            value = update_ref[place[pair * 2 + which]].astype(jnp.float32)
            turned = jnp.concatenate([swap(block) for block in blocks_of(value)], 1)
            parts.append(value * straight + turned * crossed)
        at = pl.ds(pl.multiple_of(pair * 2 * rows, 2 * rows), 2 * rows)
        lhs[at, :] = jnp.concatenate(parts, 0).astype(jnp.bfloat16)
        return 0

    lax.fori_loop(0, subgrids // 2, lift, 0, unroll=True)
    back = jnp.dot(lhs[...], table_ref[...], preferred_element_type=jnp.float32)
    out_re = jnp.zeros((rows, width), jnp.float32)
    out_im = jnp.zeros((rows, width), jnp.float32)
    for index in range(subgrids):
        re = back[index * rows : (index + 1) * rows, :width]
        im = back[index * rows : (index + 1) * rows, width:]
        c = back_ref[0, index : index + 1, :]
        s = back_ref[1, index : index + 1, :]
        out_re = out_re + (re * c - im * s)
        out_im = out_im + (re * s + im * c)
    image_ref[0] = out_re
    image_ref[1] = out_im


def gather(value, staged, facets):
    far = min(FAR, facets)
    near = facets // far
    pieces = [staged[None]]
    for step in range(1, far):
        pairs = [(index, (index + step * near) % facets) for index in range(facets)]
        pieces.append(lax.ppermute(value, "facet", pairs)[None])
    together = jnp.concatenate(pieces, 0)
    distance = near // 2
    while distance:
        pairs = [(index, index ^ distance) for index in range(facets)]
        received = lax.ppermute(together, "facet", pairs)
        together = jnp.concatenate([together, received], 0)
        distance //= 2
    return together


VMEM = pl.BlockSpec(memory_space=pltpu.VMEM)
SMEM = pl.BlockSpec(memory_space=pltpu.SMEM)
HBM = pl.BlockSpec(memory_space=pltpu.HBM)


def in_hbm(value):
    return pltpu.with_memory_space_constraint(value, pltpu.HBM)


def call(kernel, inputs, outputs, scratch, limit=8, places=None):
    return pl.pallas_call(
        kernel,
        in_specs=inputs,
        out_specs=places or jax.tree.map(lambda _: VMEM, outputs),
        out_shape=outputs,
        scratch_shapes=scratch,
        compiler_params=pltpu.CompilerParams(vmem_limit_bytes=limit << 20),
    )


def body(facets, sky_strips, prolate, subgrid_offset, owner, observed, vis_uv, vis_count):
    _, rows, width = sky_strips.shape
    slots, _, _, total = observed.shape
    subgrids = owner.shape[0]
    modulus = width * facets
    shape = jax.ShapeDtypeStruct
    weight = prolate.reshape(1, width)
    staged, mod, turns, live = call(
        functools.partial(setup_kernel, modulus, slots),
        [HBM] * 5,
        (
            shape(sky_strips.shape, jnp.bfloat16),
            shape((2, slots, facets, width), jnp.float32),
            shape((2, facets, 2 * POINTS), jnp.float32),
            shape((slots, rows, 128), jnp.int32),
        ),
        [
            pltpu.SMEM((subgrids,), jnp.int32),
            pltpu.SMEM((subgrids,), jnp.int32),
            pltpu.SMEM((slots,), jnp.int32),
            pltpu.VMEM((1, width), jnp.float32),
            pltpu.SemaphoreType.DMA((5,)),
        ],
    )(*(in_hbm(value) for value in (sky_strips, owner, subgrid_offset, vis_count, weight)))
    table = call(
        functools.partial(table_kernel, modulus),
        [],
        shape((2 * width, 2 * POINTS), jnp.bfloat16),
        [pltpu.VMEM((STEP, 2 * POINTS), jnp.float32)] * 2
        + [pltpu.VMEM((width // STEP, 2 * POINTS), jnp.float32)] * 2,
    )()
    back_table = call(
        functools.partial(back_table_kernel, modulus),
        [],
        shape((2 * POINTS, 2 * width), jnp.bfloat16),
        [pltpu.VMEM((BLOCK, width), jnp.float32)] * 2 + [pltpu.VMEM((FINE, width), jnp.float32)] * 2,
    )()
    pieces = [
        call(
            functools.partial(coarse_kernel, slot),
            [VMEM],
            (shape((BLOCK, total), jnp.bfloat16), shape((2, rows, total), jnp.float32)),
            [],
        )(vis_uv)
        for slot in range(slots)
    ]
    coarse = [piece[0] for piece in pieces]
    fine = [piece[1] for piece in pieces]
    sky = gather(sky_strips, staged, facets)
    points = call(
        functools.partial(grid_kernel, facets),
        [VMEM] * 4,
        shape((slots, 2 * FINE * rows, BLOCK), jnp.bfloat16),
        [
            pltpu.VMEM((slots * facets * rows, 2 * width), jnp.bfloat16),
            pltpu.VMEM((slots * facets * rows, 2 * POINTS), jnp.float32),
        ],
        16,
    )(sky, mod, turns, table)
    residual, update = call(
        functools.partial(visibility_kernel, slots),
        [VMEM] * (3 + 2 * slots),
        (
            shape((slots, 2, rows, total), jnp.bfloat16),
            shape((slots, rows, 2 * POINTS), jnp.bfloat16),
        ),
        [],
        16,
    )(points, live, observed, *coarse, *fine)

    back, lift, residual = call(
        functools.partial(plan_kernel, modulus),
        [HBM] * 3 + [VMEM],
        (
            shape((2, subgrids, width), jnp.float32),
            shape((2, rows, 2 * POINTS), jnp.float32),
            shape(residual.shape, residual.dtype),
        ),
        [
            pltpu.SMEM((subgrids,), jnp.int32),
            pltpu.SMEM((subgrids,), jnp.int32),
            pltpu.VMEM((1, width), jnp.float32),
            pltpu.SemaphoreType.DMA((4,)),
        ],
        places=(VMEM, VMEM, HBM),
    )(in_hbm(owner), in_hbm(subgrid_offset), in_hbm(weight), residual)
    updates = gather(update, update, facets).reshape(facets * slots, rows, 2 * POINTS)
    image = call(
        functools.partial(image_kernel, facets, slots),
        [SMEM] + [VMEM] * 4,
        shape((2, rows, width), jnp.float32),
        [
            pltpu.VMEM((subgrids * rows, 2 * POINTS), jnp.bfloat16),
            pltpu.SMEM((facets,), jnp.int32),
            pltpu.SMEM((subgrids,), jnp.int32),
        ],
        16,
    )(owner, updates, back, lift, back_table)
    return residual, image


def local(facets, *arguments):
    return body(facets, *arguments)


def solution(mesh):
    in_specs = (
        P(None, "groups", "facet"),
        P(),
        P(),
        P(),
        P(("groups", "facet"), None, None, None),
        P(("groups", "facet"), None),
        P(("groups", "facet")),
    )
    out_specs = (P(("groups", "facet"), None, None, None), P(None, "groups", "facet"))
    return jax.shard_map(
        functools.partial(local, mesh.shape["facet"]),
        mesh=mesh,
        in_specs=in_specs,
        out_specs=out_specs,
        check_vma=False,
    )
```

time: 69.6 us -> 42.7 us (0.61)
  local copies, waits for them, and re-layouts: 16.1 us -> 0.14 us
  waiting for transfers between devices: 17.6 us -> 12 us
  Pallas kernels: 19.8 us -> 15.2 us
  other arithmetic: 2.37 us -> 0.04 us
  starting transfers between devices: 12.3 us -> 14.2 us
    unnamed x36 -> x14, local copies, waits for them, and re-layouts: 16 us -> 0.06 us
    ppermute x8 -> x10, waiting for transfers between devices: 17.6 us -> 12 us  [the longest x4 6.84 us: gather(): received = lax.ppermute(together, 'facet', pairs)]
    pallas_call x3 -> x9, Pallas kernels: 19.8 us -> 15.2 us  [the longest x1 3.07 us: body(): call(functools.partial(visibility_kernel, slots), [VMEM] * (3 + 2 * slots...]
    concatenate x6 -> x2, other arithmetic: 2.37 us -> 0.04 us  [gather(): together = jnp.concatenate(pieces, 0)]
    ppermute x8 -> x10, starting transfers between devices: 12.3 us -> 14.2 us  [the longest x6 10.9 us: gather(): pieces.append(lax.ppermute(value, 'facet', pairs)[None])]
  transfers between devices with their start and end apart: 8 -> 10, of which waited for: 7 -> 7; matrix products, arithmetic and copies ran while one was open for 1% -> 0% of each run, Pallas kernels for 6% -> 20%
where the time goes in v2:
time: 42.7 us; the launch traced here: 42.5 us
  Pallas kernels  15.2 us (36%)
  starting transfers between devices  14.2 us (33%)
  waiting for transfers between devices  12 us (28%)
  between operations  0.83 us (2%)
    ppermute x6, starting transfers between devices, gather(): pieces.append(lax.ppermute(value, 'facet', pairs)[None])  10.9 us
    ppermute x4, waiting for transfers between devices, gather(): received = lax.ppermute(together, 'facet', pairs)  6.84 us
    ppermute x6, waiting for transfers between devices, gather(): pieces.append(lax.ppermute(value, 'facet', pairs)[None])  5.2 us
    ppermute x4, starting transfers between devices, gather(): received = lax.ppermute(together, 'facet', pairs)  3.31 us
    pallas_call x1, Pallas kernels, body(): call(functools.partial(visibility_kernel, slots), [VMEM] * (3 + 2 * slots...  3.07 us
    pallas_call x2, Pallas kernels, body(): call(functools.partial(coarse_kernel, slot), [VMEM], (shape((BLOCK, total...  2.67 us
    pallas_call x1, Pallas kernels, body(): call(functools.partial(image_kernel, facets, slots), [SMEM] + [VMEM] * 4,...  2.24 us
    pallas_call x1, Pallas kernels, body(): call(functools.partial(table_kernel, modulus), [], shape((2 * width, 2 *...  1.78 us
  transfers between devices with their start and end apart: 10, of which 7 were waited for; matrix products, arithmetic and copies ran while one was open for 0% of the time, Pallas kernels for 20%

profile of v2, /device:TPU:0, one launch (start us, length us, event | category | flops | bytes accessed | tf_op | source)
XLA Modules:
  0.0 42.5 jit_solution(12972621983717620570)
XLA Ops:
  0.6 0.0 copy-start.1
  0.6 3.1 %collective-permute-start = (bf16[2,8,1024]{2,1,0:T(8,128)(2,1)}, bf16[2,8,1024]{2,1,0:T(8,128)(2,1)S(1)}, u32[]{:S(2)}, u32[]{:S(2)}) collective-permute-start(bf16[2,8,1024]{2,1,0:T(8,128)(2,1)} %sky_hbm.1), channel_id=1, source_target_pairs={{0,4},{1,5},{2,6},{3,7},{4,8},{5,9},{6,10},{7,11},{8,12},{9,13},{1... | collective-permute-start | bytes 98312 | tf_op jit(solution)/shard_map/ppermute | solution.py:445
  3.7 2.6 %collective-permute-start.1 = (bf16[2,8,1024]{2,1,0:T(8,128)(2,1)}, bf16[2,8,1024]{2,1,0:T(8,128)(2,1)S(1)}, u32[]{:S(2)}, u32[]{:S(2)}) collective-permute-start(bf16[2,8,1024]{2,1,0:T(8,128)(2,1)} %sky_hbm.1), channel_id=1, source_target_pairs={{0,8},{1,9},{2,10},{3,11},{4,12},{5,13},{6,14},{7,15},{8,0},{9,1},... | collective-permute-start | bytes 98312 | tf_op jit(solution)/shard_map/ppermute | solution.py:445
  6.3 1.3 %collective-permute-start.2 = (bf16[2,8,1024]{2,1,0:T(8,128)(2,1)}, bf16[2,8,1024]{2,1,0:T(8,128)(2,1)S(1)}, u32[]{:S(2)}, u32[]{:S(2)}) collective-permute-start(bf16[2,8,1024]{2,1,0:T(8,128)(2,1)} %sky_hbm.1), channel_id=1, source_target_pairs={{0,12},{1,13},{2,14},{3,15},{4,0},{5,1},{6,2},{7,3},{8,4},{9,5},{1... | collective-permute-start | bytes 98312 | tf_op jit(solution)/shard_map/ppermute | solution.py:445
  7.7 1.3 %shard_map.86 = (bf16[2,8,1024]{2,1,0:T(8,128)(2,1)S(1)}, f32[2,2,16,1024]{3,2,1,0:T(8,128)S(1)}, f32[2,16,1024]{2,1,0:T(8,128)S(1)}, s32[2,8,128]{2,1,0:T(8,128)S(1)}) custom-call(bf16[2,8,1024]{2,1,0:T(8,128)(2,1)} %sky_hbm.1, s32[16]{0:T(128)} %owner_ref.1, s32[16]{0:T(128)} %offset_hbm.3, s32[2]{0:T(128)} %count_hbm.1, f32[1,1024]{1,0:T(1,128)} %bitcast.35), custom_call_target="tpu_custom_call" | custom-call | tf_op jit(solution)/shard_map/pallas_call | solution.py:483
  9.0 0.0 collective-permute-done
  9.0 0.1 collective-permute-done.1
  9.1 1.3 %collective-permute-done.2 = bf16[2,8,1024]{2,1,0:T(8,128)(2,1)S(1)} collective-permute-done((bf16[2,8,1024]{2,1,0:T(8,128)(2,1)}, bf16[2,8,1024]{2,1,0:T(8,128)(2,1)S(1)}, u32[]{:S(2)}, u32[]{:S(2)}) %collective-permute-start.2) | collective-permute-done | bytes 32800 | tf_op jit(solution)/shard_map/ppermute | solution.py:445
  10.5 1.6 %collective-permute-start.3 = (bf16[4,2,8,1024]{3,2,1,0:T(8,128)(2,1)S(1)}, bf16[4,2,8,1024]{3,2,1,0:T(8,128)(2,1)S(1)}, u32[]{:S(2)}, u32[]{:S(2)}) collective-permute-start(bf16[4,2,8,1024]{3,2,1,0:T(8,128)(2,1)S(1)} %pad_maximum_fusion), channel_id=1, source_target_pairs={{0,2},{1,3},{2,0},{3,1},{4,6},{5,7},{6,4},{7,5},{8,10},{9,11},{10,... | collective-permute-start | bytes 393224 | tf_op jit(solution)/shard_map/ppermute | solution.py:450
  12.1 3.4 %collective-permute-done.3 = bf16[4,2,8,1024]{3,2,1,0:T(8,128)(2,1)S(1)} collective-permute-done((bf16[4,2,8,1024]{3,2,1,0:T(8,128)(2,1)S(1)}, bf16[4,2,8,1024]{3,2,1,0:T(8,128)(2,1)S(1)}, u32[]{:S(2)}, u32[]{:S(2)}) %collective-permute-start.3) | collective-permute-done | bytes 131104 | tf_op jit(solution)/shard_map/ppermute | solution.py:450
  15.5 0.0 copy-start
  15.6 0.1 collective-permute-start.4
  15.6 1.8 %shard_map.87.table_ref = bf16[2048,1024]{1,0:T(8,128)(2,1)S(1)} custom-call(), custom_call_target="tpu_custom_call" | custom-call | tf_op jit(solution)/shard_map/pallas_call | solution.py:500
  17.4 0.0 copy-done.1
  17.4 1.3 %shard_map.89 = (bf16[128,8192]{1,0:T(8,128)(2,1)S(1)}, f32[2,8,8192]{2,1,0:T(8,128)S(1)}) custom-call(f32[2,8192]{1,0:T(2,128)S(1)} %copy-done.1), custom_call_target="tpu_custom_call" | custom-call | tf_op jit(solution)/shard_map/pallas_call | solution.py:514
  18.8 1.3 %shard_map.90 = (bf16[128,8192]{1,0:T(8,128)(2,1)S(1)}, f32[2,8,8192]{2,1,0:T(8,128)S(1)}) custom-call(f32[2,8192]{1,0:T(2,128)S(1)} %copy-done.1), custom_call_target="tpu_custom_call" | custom-call | tf_op jit(solution)/shard_map/pallas_call | solution.py:514
  20.1 0.0 collective-permute-done.4
  20.1 1.5 %shard_map.88.points_ref = bf16[2,128,128]{2,1,0:T(8,128)(2,1)S(1)} custom-call(bf16[16,2,8,1024]{3,2,1,0:T(8,128)(2,1)S(1)} %constant_dynamic-update-slice_fusion.5.sky_ref, f32[2,2,16,1024]{3,2,1,0:T(8,128)S(1)} %get-tuple-element.16.mod_ref, f32[2,16,1024]{2,1,0:T(8,128)S(1)} %get-tuple-element.17.turn_ref, bf16[2048,1024]{1,0:T(8,128)(2,1)S(1)} %shard_map.87.table_ref), custom_call_target="tpu_custom_call" | custom-call | tf_op jit(solution)/shard_map/pallas_call | solution.py:525
  21.7 0.0 copy-done
  21.7 3.1 %shard_map.91 = (bf16[2,2,8,8192]{3,2,1,0:T(8,128)(2,1)S(1)}, bf16[2,8,1024]{2,1,0:T(8,128)(2,1)S(1)}) custom-call(bf16[2,128,128]{2,1,0:T(8,128)(2,1)S(1)} %shard_map.88.points_ref, s32[2,8,128]{2,1,0:T(8,128)S(1)} %get-tuple-element.18.live_ref, f32[2,2,8,8192]{3,2,1,0:T(8,128)S(1)} %copy-done, bf16[128,8192]{1,0:T(8,128)(2,1)S(1)} %get-tuple-element.19.refs_0_, ...), custom_call_target="tpu_custom_call" | custom-call | tf_op jit(solution)/shard_map/pallas_call | solution.py:535
  24.7 0.0 copy-start.2
  24.7 0.3 collective-permute-start.5
  25.0 3.5 %collective-permute-start.6 = (bf16[2,8,1024]{2,1,0:T(8,128)(2,1)S(1)}, bf16[2,8,1024]{2,1,0:T(8,128)(2,1)S(1)}, u32[]{:S(2)}, u32[]{:S(2)}) collective-permute-start(bf16[2,8,1024]{2,1,0:T(8,128)(2,1)S(1)} %get-tuple-element.25), channel_id=1, source_target_pairs={{0,8},{1,9},{2,10},{3,11},{4,12},{5,13},{6,14},{7,15},{8,0},{9,1},... | collective-permute-start | bytes 98312 | tf_op jit(solution)/shard_map/ppermute | solution.py:445
  28.5 0.1 collective-permute-start.7
  28.6 2.2 %collective-permute-done.5 = bf16[2,8,1024]{2,1,0:T(8,128)(2,1)S(1)} collective-permute-done((bf16[2,8,1024]{2,1,0:T(8,128)(2,1)S(1)}, bf16[2,8,1024]{2,1,0:T(8,128)(2,1)S(1)}, u32[]{:S(2)}, u32[]{:S(2)}) %collective-permute-start.5) | collective-permute-done | bytes 32800 | tf_op jit(solution)/shard_map/ppermute | solution.py:445
  30.8 1.0 %collective-permute-done.6 = bf16[2,8,1024]{2,1,0:T(8,128)(2,1)S(1)} collective-permute-done((bf16[2,8,1024]{2,1,0:T(8,128)(2,1)S(1)}, bf16[2,8,1024]{2,1,0:T(8,128)(2,1)S(1)}, u32[]{:S(2)}, u32[]{:S(2)}) %collective-permute-start.6) | collective-permute-done | bytes 32800 | tf_op jit(solution)/shard_map/ppermute | solution.py:445
  31.9 0.5 %collective-permute-done.7 = bf16[2,8,1024]{2,1,0:T(8,128)(2,1)S(1)} collective-permute-done((bf16[2,8,1024]{2,1,0:T(8,128)(2,1)S(1)}, bf16[2,8,1024]{2,1,0:T(8,128)(2,1)S(1)}, u32[]{:S(2)}, u32[]{:S(2)}) %collective-permute-start.7) | collective-permute-done | bytes 32800 | tf_op jit(solution)/shard_map/ppermute | solution.py:445
  32.4 1.6 %collective-permute-start.8 = (bf16[4,2,8,1024]{3,2,1,0:T(8,128)(2,1)S(1)}, bf16[4,2,8,1024]{3,2,1,0:T(8,128)(2,1)S(1)}, u32[]{:S(2)}, u32[]{:S(2)}) collective-permute-start(bf16[4,2,8,1024]{3,2,1,0:T(8,128)(2,1)S(1)} %pad_maximum_fusion.1), channel_id=1, source_target_pairs={{0,2},{1,3},{2,0},{3,1},{4,6},{5,7},{6,4},{7,5},{8,10},{9,11},{10,... | collective-permute-start | bytes 393224 | tf_op jit(solution)/shard_map/ppermute | solution.py:450
  34.1 3.4 %collective-permute-done.8 = bf16[4,2,8,1024]{3,2,1,0:T(8,128)(2,1)S(1)} collective-permute-done((bf16[4,2,8,1024]{3,2,1,0:T(8,128)(2,1)S(1)}, bf16[4,2,8,1024]{3,2,1,0:T(8,128)(2,1)S(1)}, u32[]{:S(2)}, u32[]{:S(2)}) %collective-permute-start.8) | collective-permute-done | bytes 131104 | tf_op jit(solution)/shard_map/ppermute | solution.py:450
  37.5 0.1 collective-permute-start.9
  37.6 1.7 %shard_map.93.table_ref = bf16[1024,2048]{1,0:T(8,128)(2,1)S(1)} custom-call(), custom_call_target="tpu_custom_call" | custom-call | tf_op jit(solution)/shard_map/pallas_call | solution.py:507
  39.3 0.9 %shard_map.92 = (f32[2,16,1024]{2,1,0:T(8,128)S(1)}, f32[2,8,1024]{2,1,0:T(8,128)S(1)}, bf16[2,2,8,8192]{3,2,1,0:T(8,128)(2,1)}) custom-call(s32[16]{0:T(128)} %owner_ref.1, s32[16]{0:T(128)} %offset_hbm.3, f32[1,1024]{1,0:T(1,128)} %bitcast.36, bf16[2,2,8,8192]{3,2,1,0:T(8,128)(2,1)S(1)} %get-tuple-element.23.residual_ref), custom_call_target="tpu_custom_call" | custom-call | tf_op jit(solution)/shard_map/pallas_call | solution.py:546
  40.2 0.0 collective-permute-done.9
  40.2 0.0 copy-done.2
  40.2 2.2 %shard_map.94 = f32[2,8,1024]{2,1,0:T(8,128)} custom-call(s32[16]{0:T(128)S(1)} %copy-done.2, bf16[32,8,1024]{2,1,0:T(8,128)(2,1)S(1)} %bitcast.26, f32[2,16,1024]{2,1,0:T(8,128)S(1)} %get-tuple-element.26.back_ref, f32[2,8,1024]{2,1,0:T(8,128)S(1)} %get-tuple-element.27.lift_ref, bf16[1024,2048]{1,0:T(8,128)(2,1)S(1)} %shard_map.93.table_ref), custom_call_target="tpu_custom_call" | custom-call | tf_op jit(solution)/shard_map/pallas_call | solution.py:563
  (14 shorter events, 0.2 us)
Async XLA Ops:
  0.6 16.8 %copy-start.1 = (f32[2,8192]{1,0:T(2,128)S(1)}, f32[2,8192]{1,0:T(2,128)}, u32[]{:S(2)}) copy-start(f32[2,8192]{1,0:T(2,128)} %uv_ref.3) | copy-start | bytes 196612
  0.6 8.4 %collective-permute-start = (bf16[2,8,1024]{2,1,0:T(8,128)(2,1)}, bf16[2,8,1024]{2,1,0:T(8,128)(2,1)S(1)}, u32[]{:S(2)}, u32[]{:S(2)}) collective-permute-start(bf16[2,8,1024]{2,1,0:T(8,128)(2,1)} %sky_hbm.1), channel_id=1, source_target_pairs={{0,4},{1,5},{2,6},{3,7},{4,8},{5,9},{6,10},{7,11},{8,12},{9,13},{1... | collective-permute-start | bytes 98312 | tf_op jit(solution)/shard_map/ppermute | solution.py:445
  3.7 5.4 %collective-permute-start.1 = (bf16[2,8,1024]{2,1,0:T(8,128)(2,1)}, bf16[2,8,1024]{2,1,0:T(8,128)(2,1)S(1)}, u32[]{:S(2)}, u32[]{:S(2)}) collective-permute-start(bf16[2,8,1024]{2,1,0:T(8,128)(2,1)} %sky_hbm.1), channel_id=1, source_target_pairs={{0,8},{1,9},{2,10},{3,11},{4,12},{5,13},{6,14},{7,15},{8,0},{9,1},... | collective-permute-start | bytes 98312 | tf_op jit(solution)/shard_map/ppermute | solution.py:445
  6.3 4.1 %collective-permute-start.2 = (bf16[2,8,1024]{2,1,0:T(8,128)(2,1)}, bf16[2,8,1024]{2,1,0:T(8,128)(2,1)S(1)}, u32[]{:S(2)}, u32[]{:S(2)}) collective-permute-start(bf16[2,8,1024]{2,1,0:T(8,128)(2,1)} %sky_hbm.1), channel_id=1, source_target_pairs={{0,12},{1,13},{2,14},{3,15},{4,0},{5,1},{6,2},{7,3},{8,4},{9,5},{1... | collective-permute-start | bytes 98312 | tf_op jit(solution)/shard_map/ppermute | solution.py:445
  10.5 5.0 %collective-permute-start.3 = (bf16[4,2,8,1024]{3,2,1,0:T(8,128)(2,1)S(1)}, bf16[4,2,8,1024]{3,2,1,0:T(8,128)(2,1)S(1)}, u32[]{:S(2)}, u32[]{:S(2)}) collective-permute-start(bf16[4,2,8,1024]{3,2,1,0:T(8,128)(2,1)S(1)} %pad_maximum_fusion), channel_id=1, source_target_pairs={{0,2},{1,3},{2,0},{3,1},{4,6},{5,7},{6,4},{7,5},{8,10},{9,11},{10,... | collective-permute-start | bytes 393224 | tf_op jit(solution)/shard_map/ppermute | solution.py:450
  15.5 6.1 %copy-start = (f32[2,2,8,8192]{3,2,1,0:T(8,128)S(1)}, f32[2,2,8,8192]{3,2,1,0:T(8,128)}, u32[]{:S(2)}) copy-start(f32[2,2,8,8192]{3,2,1,0:T(8,128)} %observed_ref.1) | copy-start | bytes 3145732
  15.6 4.6 %collective-permute-start.4 = (bf16[8,2,8,1024]{3,2,1,0:T(8,128)(2,1)S(1)}, bf16[8,2,8,1024]{3,2,1,0:T(8,128)(2,1)S(1)}, u32[]{:S(2)}, u32[]{:S(2)}) collective-permute-start(bf16[8,2,8,1024]{3,2,1,0:T(8,128)(2,1)S(1)} %get-tuple-element.30), channel_id=1, source_target_pairs={{0,1},{1,0},{2,3},{3,2},{4,5},{5,4},{6,7},{7,6},{8,9},{9,8},{10,11... | collective-permute-start | bytes 786440 | tf_op jit(solution)/shard_map/ppermute | solution.py:450
  24.7 15.5 %copy-start.2 = (s32[16]{0:T(128)S(1)}, s32[16]{0:T(128)}, u32[]{:S(2)}) copy-start(s32[16]{0:T(128)} %owner_ref.1) | copy-start | bytes 196
  24.7 6.1 %collective-permute-start.5 = (bf16[2,8,1024]{2,1,0:T(8,128)(2,1)S(1)}, bf16[2,8,1024]{2,1,0:T(8,128)(2,1)S(1)}, u32[]{:S(2)}, u32[]{:S(2)}) collective-permute-start(bf16[2,8,1024]{2,1,0:T(8,128)(2,1)S(1)} %get-tuple-element.25), channel_id=1, source_target_pairs={{0,4},{1,5},{2,6},{3,7},{4,8},{5,9},{6,10},{7,11},{8,12},{9,13},{1... | collective-permute-start | bytes 98312 | tf_op jit(solution)/shard_map/ppermute | solution.py:445
  25.0 6.8 %collective-permute-start.6 = (bf16[2,8,1024]{2,1,0:T(8,128)(2,1)S(1)}, bf16[2,8,1024]{2,1,0:T(8,128)(2,1)S(1)}, u32[]{:S(2)}, u32[]{:S(2)}) collective-permute-start(bf16[2,8,1024]{2,1,0:T(8,128)(2,1)S(1)} %get-tuple-element.25), channel_id=1, source_target_pairs={{0,8},{1,9},{2,10},{3,11},{4,12},{5,13},{6,14},{7,15},{8,0},{9,1},... | collective-permute-start | bytes 98312 | tf_op jit(solution)/shard_map/ppermute | solution.py:445
  28.5 3.9 %collective-permute-start.7 = (bf16[2,8,1024]{2,1,0:T(8,128)(2,1)S(1)}, bf16[2,8,1024]{2,1,0:T(8,128)(2,1)S(1)}, u32[]{:S(2)}, u32[]{:S(2)}) collective-permute-start(bf16[2,8,1024]{2,1,0:T(8,128)(2,1)S(1)} %get-tuple-element.25), channel_id=1, source_target_pairs={{0,12},{1,13},{2,14},{3,15},{4,0},{5,1},{6,2},{7,3},{8,4},{9,5},{1... | collective-permute-start | bytes 98312 | tf_op jit(solution)/shard_map/ppermute | solution.py:445
  32.4 5.0 %collective-permute-start.8 = (bf16[4,2,8,1024]{3,2,1,0:T(8,128)(2,1)S(1)}, bf16[4,2,8,1024]{3,2,1,0:T(8,128)(2,1)S(1)}, u32[]{:S(2)}, u32[]{:S(2)}) collective-permute-start(bf16[4,2,8,1024]{3,2,1,0:T(8,128)(2,1)S(1)} %pad_maximum_fusion.1), channel_id=1, source_target_pairs={{0,2},{1,3},{2,0},{3,1},{4,6},{5,7},{6,4},{7,5},{8,10},{9,11},{10,... | collective-permute-start | bytes 393224 | tf_op jit(solution)/shard_map/ppermute | solution.py:450
  37.5 2.7 %collective-permute-start.9 = (bf16[8,2,8,1024]{3,2,1,0:T(8,128)(2,1)S(1)}, bf16[8,2,8,1024]{3,2,1,0:T(8,128)(2,1)S(1)}, u32[]{:S(2)}, u32[]{:S(2)}) collective-permute-start(bf16[8,2,8,1024]{3,2,1,0:T(8,128)(2,1)S(1)} %get-tuple-element.28), channel_id=1, source_target_pairs={{0,1},{1,0},{2,3},{3,2},{4,5},{5,4},{6,7},{7,6},{8,9},{9,8},{10,11... | collective-permute-start | bytes 786440 | tf_op jit(solution)/shard_map/ppermute | solution.py:450

commit v3 on v2

v3 whole, which is shorter than its diff:
```python
import functools
import math

import jax
import jax.numpy as jnp
from jax import lax
from jax.experimental import pallas as pl
from jax.experimental.pallas import tpu as pltpu
from jax.sharding import PartitionSpec as P


POINTS = 512
FINE = 8
COARSE = POINTS // FINE
BLOCK = 2 * COARSE
ROOT = 8
SPLIT = 2
STEP = 64
FAR = 4
CHUNK = 512

COS = (
    0.9999999890590217, -4.934801124863452, 4.058694841243232, -1.3351584301691248,
    0.23502980840046309, -0.025358983639642813, 0.001593910683444594,
)
SIN = (
    3.14159265125575, -5.167712550664621, 2.550160355805489, -0.5992423074495862,
    0.08208188864038139, -0.00727531575291481, 0.00039528045693413335,
)


def horner(coefficients, z):
    total = coefficients[-1] * z + coefficients[-2]
    for value in coefficients[-3::-1]:
        total = total * z + value
    return total


def turn(t):
    y = 2.0 * (t - jnp.floor(t + 0.5))
    z = y * y
    return horner(COS, z), horner(SIN, z) * y


def modular(first, second, modulus):
    if modulus & (modulus - 1) == 0:
        return (first * second) & (modulus - 1)
    upper = second // 256
    lower = second % 256
    return (first * lower % modulus + first * upper % modulus * 256 % modulus) % modulus


def iota(shape, axis):
    return lax.broadcasted_iota(jnp.int32, shape, axis)


def column_points(shape):
    column = iota(shape, 1)
    return (column % COARSE) * FINE + column // BLOCK, (column // COARSE) % 2


def position_of(facet, me, facets):
    far = min(FAR, facets)
    near = facets // far
    bits = near.bit_length() - 1
    flipped = facet * 0
    for bit in range(bits):
        flipped = flipped | ((((facet ^ me) >> bit) & 1) << (bits - 1 - bit))
    return (me // near - facet // near + far) % far + far * flipped


def swap(block):
    return pltpu.roll(block, COARSE, 1)


def blocks_of(value):
    return [value[:, b * BLOCK : (b + 1) * BLOCK] for b in range(FINE)]


def find_offsets(me, owner_ref, offset_ref, slots):
    def find(index, carry):
        held, offsets = carry
        mine = owner_ref[index] == me
        offsets = tuple(
            jnp.where(mine & (held == slot), offset_ref[index], offsets[slot]) for slot in range(slots)
        )
        return held + mine.astype(jnp.int32), offsets

    zero = jnp.int32(0)
    return lax.fori_loop(0, owner_ref.shape[0], find, (zero, (zero,) * slots))


def fraction_of(first, second, modulus):
    return modular(first, second, modulus).astype(jnp.float32) * (1.0 / modulus)


def fetch(copies, semaphores):
    started = [
        pltpu.make_async_copy(source, target, semaphores.at[index])
        for index, (source, target) in enumerate(copies)
    ]
    for copy in started:
        copy.start()
    return started


def wait_for(copies):
    for copy in copies:
        copy.wait()


def setup_kernel(
    modulus,
    slots,
    owner_hbm,
    offset_hbm,
    count_hbm,
    prolate_hbm,
    sky_hbm,
    uv_hbm,
    observed_hbm,
    mod_ref,
    turn_ref,
    live_ref,
    sky_ref,
    uv_ref,
    observed_ref,
    owner_ref,
    offset_ref,
    count_ref,
    prolate_ref,
    semaphores,
):
    copies = fetch(
        (
            (owner_hbm, owner_ref),
            (offset_hbm, offset_ref),
            (count_hbm, count_ref),
            (prolate_hbm, prolate_ref),
            (sky_hbm, sky_ref),
            (uv_hbm, uv_ref),
            (observed_hbm, observed_ref),
        ),
        semaphores,
    )
    wait_for(copies[:4])
    me = lax.axis_index("facet")
    facets, width = mod_ref.shape[2:]
    held, offsets = find_offsets(me, owner_ref, offset_ref, slots)
    weight = prolate_ref[...]

    across = iota((facets, width), 0) * width + iota((facets, width), 1)
    for slot in range(slots):
        c, s = turn(fraction_of(across, offsets[slot], modulus))
        mod_ref[0, slot] = c * weight
        mod_ref[1, slot] = s * weight
        live_ref[slot] = jnp.full(live_ref.shape[1:], jnp.where(slot < held, count_ref[slot], 0))

    points, part = column_points(turn_ref.shape[1:])
    c, s = turn(fraction_of(iota(points.shape, 0), points, facets * SPLIT))
    scale = 1.0 / math.sqrt(modulus)
    turn_ref[0] = c * scale
    turn_ref[1] = jnp.where(part == 0, -s, s) * scale
    wait_for(copies[4:])


def plan_kernel(
    modulus,
    owner_hbm,
    offset_hbm,
    prolate_hbm,
    residual_ref,
    back_ref,
    lift_ref,
    residual_hbm,
    owner_ref,
    offset_ref,
    prolate_ref,
    semaphores,
):
    leaving = pltpu.make_async_copy(residual_ref, residual_hbm, semaphores.at[3])
    leaving.start()
    wait_for(
        fetch(
            ((owner_hbm, owner_ref), (offset_hbm, offset_ref), (prolate_hbm, prolate_ref)), semaphores
        )
    )
    me = lax.axis_index("facet")
    facets = lax.axis_size("facet")
    subgrids, width = back_ref.shape[1:]
    row = iota((subgrids, 128), 0)

    def place_offset(index, placed):
        return jnp.where(row == index, offset_ref[index], placed)

    column = lax.fori_loop(0, subgrids, place_offset, jnp.zeros(row.shape, jnp.int32), unroll=True)
    across = me * width + iota((subgrids, width), 1)
    c, s = turn(fraction_of(across, jnp.concatenate([column] * (width // 128), 1), modulus))
    weight = prolate_ref[...] * (1.0 / math.sqrt(subgrids * POINTS))
    back_ref[0] = c * weight
    back_ref[1] = s * weight

    points, part = column_points(lift_ref.shape[1:])
    c, s = turn(fraction_of(me * SPLIT + iota(points.shape, 0), points, facets * SPLIT))
    lift_ref[0] = c
    lift_ref[1] = jnp.where(part == 0, -s, s)
    leaving.wait()


def table_kernel(modulus, table_ref, v_re, v_im, u_re, u_im):
    width = table_ref.shape[0] // 2
    points, part = column_points(v_re.shape)
    fraction = fraction_of(iota(v_re.shape, 0), points, modulus)
    v_re[...], v_im[...] = turn(fraction + 0.25 * part.astype(jnp.float32))
    points, _ = column_points(u_re.shape)
    u_re[...], u_im[...] = turn(fraction_of(iota(u_re.shape, 0) * STEP, points, modulus))

    def table_step(step, _):
        c = u_re[pl.ds(step, 1), :]
        s = u_im[pl.ds(step, 1), :]
        row = pl.multiple_of(step * STEP, STEP)
        table_ref[pl.ds(row, STEP), :] = (v_re[...] * c - v_im[...] * s).astype(jnp.bfloat16)
        table_ref[pl.ds(width + row, STEP), :] = (v_re[...] * s + v_im[...] * c).astype(jnp.bfloat16)
        return 0

    lax.fori_loop(0, width // STEP, table_step, 0)


def back_table_kernel(modulus, table_ref, v_re, v_im, u_re, u_im):
    width = table_ref.shape[1] // 2
    row = iota(v_re.shape, 0)
    fraction = fraction_of(iota(v_re.shape, 1), row % COARSE * FINE, modulus)
    v_re[...], v_im[...] = turn(fraction + 0.25 * (row // COARSE).astype(jnp.float32))
    u_re[...], u_im[...] = turn(fraction_of(iota(u_re.shape, 1), iota(u_re.shape, 0), modulus))

    def table_step(b, _):
        c = u_re[pl.ds(b, 1), :]
        s = u_im[pl.ds(b, 1), :]
        at = pl.ds(pl.multiple_of(b * BLOCK, BLOCK), BLOCK)
        table_ref[at, :width] = (v_re[...] * c - v_im[...] * s).astype(jnp.bfloat16)
        table_ref[at, width:] = (v_re[...] * s + v_im[...] * c).astype(jnp.bfloat16)
        return 0

    lax.fori_loop(0, FINE, table_step, 0)


def combine(products, rows, halves):
    count = products.shape[0] // (2 * rows)
    return [
        swap(products[(count + b) * rows : (count + b + 1) * rows]) + products[b * rows : (b + 1) * rows] * halves
        for b in range(count)
    ]


def split(value):
    part = value.shape[1] // SPLIT
    return jnp.concatenate([value[:, index * part : (index + 1) * part] for index in range(SPLIT)], 0)


def half_signs(rows):
    return jnp.where(iota((rows, BLOCK), 1) < COARSE, jnp.float32(1.0), jnp.float32(-1.0))


def powers(c, s, bits):
    re = jnp.where(bits[0], c, 1.0)
    im = jnp.where(bits[0], s, 0.0)
    for bit in bits[1:]:
        c, s = c * c - s * s, 2.0 * c * s
        re, im = (
            jnp.where(bit, re * c - im * s, re),
            jnp.where(bit, re * s + im * c, im),
        )
    return re, im


def observe_kernel(
    slot, uv_ref, live_ref, observed_ref, coarse_ref, fine_ref, seen_ref, lags_ref, step_c, step_s, back_c, back_s, root_c, root_s, packed
):
    count, wide = packed.shape
    rows = observed_ref.shape[2]
    for row in range(count):
        packed[row : row + 1, :] = uv_ref[slot : slot + 1, row * wide : (row + 1) * wide]
    u = packed[...]
    fine_ref[0], fine_ref[1] = turn(u * (1.0 / POINTS))
    step_c[...], step_s[...] = turn(u * (FINE * ROOT / POINTS))
    back_c[...], back_s[...] = turn(u)
    root_c[...], root_s[...] = turn(u * (FINE / POINTS))
    chunk = min(CHUNK, wide)
    bits = [(iota((ROOT, chunk), 0) >> bit) % 2 == 1 for bit in range(3)]
    live = jnp.concatenate([live_ref[slot]] * (chunk // live_ref.shape[2]), 1)
    gathered = jnp.zeros((2 * FINE * (rows + 2), BLOCK), jnp.float32)

    for row in range(count):
        for start in range(0, wide, chunk):
            here = slice(start, start + chunk)
            at = slice(row * wide + start, row * wide + start + chunk)

            def spread(ref):
                return jnp.broadcast_to(ref[row : row + 1, here], (ROOT, chunk))

            re, im = powers(spread(root_c), spread(root_s), bits)
            c, s = spread(step_c), spread(step_s)
            cosines, sines = [], []
            for step in range(ROOT):
                cosines.append(re)
                sines.append(im)
                if step + 1 < ROOT:
                    re, im = re * c - im * s, re * s + im * c
            coarse = jnp.concatenate(cosines + sines, 0).astype(jnp.bfloat16)
            coarse_ref[:, at] = coarse

            alive = row * wide + start + iota((rows, chunk), 1) < live
            c = jnp.broadcast_to(fine_ref[0, row : row + 1, here], (rows, chunk))
            s = jnp.broadcast_to(fine_ref[1, row : row + 1, here], (rows, chunk))
            re = jnp.where(alive, observed_ref[slot, 0, :, at], 0.0)
            im = jnp.where(alive, observed_ref[slot, 1, :, at], 0.0)
            all_re, all_im = [re], [im]
            for _ in range(1, FINE):
                re, im = re * c + im * s, im * c - re * s
                all_re.append(re)
                all_im.append(im)
            re, im = powers(c, -s, bits)
            re = jnp.where(alive, re, 0.0)
            im = jnp.where(alive, im, 0.0)
            c, s = spread(back_c), spread(back_s)
            all_re += [re * c - im * s, re]
            all_im += [re * s + im * c, im]
            gathered = gathered + lax.dot_general(
                jnp.concatenate(all_re + all_im, 0).astype(jnp.bfloat16),
                coarse,
                (((1,), (1,)), ((), ())),
                preferred_element_type=jnp.float32,
            )

    blocks = combine(gathered, rows, half_signs(rows))
    for b in range(FINE):
        seen_ref[:, b * BLOCK : (b + 1) * BLOCK] = blocks[b]
    before, after = blocks[FINE:]
    first = iota((FINE, BLOCK), 1) < COARSE
    lags_ref[0] = jnp.where(first, before, swap(after))
    lags_ref[1] = jnp.where(first, swap(before), after)


def toeplitz_kernel(slots, *refs):
    first = iota((COARSE, BLOCK), 1) < COARSE

    def slant(ref, part, row, shift):
        line = jnp.broadcast_to(ref[part, row : row + 1, :], (COARSE, BLOCK))
        return pltpu.roll(line, shift, 1, stride=1, stride_axis=0)

    for slot in range(slots):
        lags_ref, matrix_ref = refs[slot], refs[slots + slot]
        for place in range(2 * FINE - 1):
            beta = place - (FINE - 1)
            row, late = (beta, 0) if beta >= 0 else (beta + FINE, 1)
            upper = jnp.where(
                first, slant(lags_ref, 0, row, COARSE + late), slant(lags_ref, 1, row, late)
            )
            lower = jnp.where(
                first, -slant(lags_ref, 1, row, COARSE + late), slant(lags_ref, 0, row, late)
            )
            value = jnp.concatenate([upper, lower], 0)
            high = value.astype(jnp.bfloat16)
            at = slice(place * BLOCK, (place + 1) * BLOCK)
            matrix_ref[:BLOCK, at] = high
            matrix_ref[BLOCK:, at] = (value - high.astype(jnp.float32)).astype(jnp.bfloat16)
        matrix_ref[:, (2 * FINE - 1) * BLOCK :] = jnp.zeros((2 * BLOCK, BLOCK), jnp.bfloat16)


def grid_kernel(facets, total, sky_ref, mod_ref, turn_ref, table_ref, *refs):
    me = lax.axis_index("facet")
    slots = mod_ref.shape[1]
    seen_refs, matrix_refs = refs[:slots], refs[slots : 2 * slots]
    points_ref, update_ref, lhs, raw = refs[2 * slots :]
    part = sky_ref.shape[3] // SPLIT
    rows = sky_ref.shape[2]

    for slot in range(slots):

        def modulate(facet, _):
            c = mod_ref[0, slot, pl.ds(facet, 1), :]
            s = mod_ref[1, slot, pl.ds(facet, 1), :]
            position = position_of(facet, me, facets)
            re = sky_ref[position, 0].astype(jnp.float32)
            im = sky_ref[position, 1].astype(jnp.float32)
            row = pl.multiple_of((slot * facets + facet) * SPLIT * rows, SPLIT * rows)
            at = pl.ds(row, SPLIT * rows)
            lhs[at, :part] = split(re * c + im * s).astype(jnp.bfloat16)
            lhs[at, part:] = split(im * c - re * s).astype(jnp.bfloat16)
            return 0

        lax.fori_loop(0, facets, modulate, 0, unroll=True)

    raw[...] = jnp.dot(lhs[...], table_ref[...], preferred_element_type=jnp.float32)
    halves = half_signs(rows)

    for slot in range(slots):

        def add_facet(position, carry):
            straight, crossed = carry
            row = pl.multiple_of((slot * facets * SPLIT + position) * rows, rows)
            value = raw[pl.ds(row, rows), :]
            return (
                straight + value * turn_ref[0, pl.ds(position, 1), :],
                crossed + value * turn_ref[1, pl.ds(position, 1), :],
            )

        empty = jnp.zeros((rows, FINE * BLOCK), jnp.float32)
        straight, crossed = lax.fori_loop(0, facets * SPLIT, add_facet, (empty, empty), unroll=True)
        grid = [
            (first + swap(second)).astype(jnp.bfloat16).astype(jnp.float32)
            for first, second in zip(blocks_of(straight), blocks_of(crossed))
        ]
        points_ref[slot] = jnp.concatenate(
            [block * halves for block in grid] + [swap(block) for block in grid], 0
        ).astype(jnp.bfloat16)

        stacked = jnp.concatenate(grid, 0).astype(jnp.bfloat16)
        products = jnp.dot(
            jnp.concatenate([stacked, stacked], 1), matrix_refs[slot][...], preferred_element_type=jnp.float32
        )
        for after in range(FINE):
            model = sum(
                products[
                    b * rows : (b + 1) * rows,
                    (after - b + FINE - 1) * BLOCK : (after - b + FINE) * BLOCK,
                ]
                for b in range(FINE)
            )
            at = slice(after * BLOCK, (after + 1) * BLOCK)
            update_ref[slot, :, at] = (
                (seen_refs[slot][:, at] - model * (1.0 / math.sqrt(POINTS))) * (1.0 / math.sqrt(total))
            ).astype(jnp.bfloat16)


def residual_kernel(slots, points_ref, live_ref, observed_ref, *refs):
    coarse_refs, fine_refs = refs[:slots], refs[slots : 2 * slots]
    residual_ref = refs[2 * slots]
    _, _, rows, total = observed_ref.shape
    chunk = min(CHUNK, total)

    for slot in range(slots):
        points_lhs = points_ref[slot]
        live = jnp.concatenate([live_ref[slot]] * (chunk // live_ref.shape[2]), 1)
        wide = fine_refs[slot].shape[2]
        for start in range(0, total, chunk):
            at = slice(start, start + chunk)
            row, here = start // wide, slice(start % wide, start % wide + chunk)
            c = jnp.broadcast_to(fine_refs[slot][0, row : row + 1, here], (rows, chunk))
            s = jnp.broadcast_to(fine_refs[slot][1, row : row + 1, here], (rows, chunk))
            terms = jnp.dot(points_lhs, coarse_refs[slot][:, at], preferred_element_type=jnp.float32)
            half = FINE * rows
            re = terms[half - rows : half]
            im = terms[2 * half - rows :]
            for b in range(FINE - 2, -1, -1):
                re, im = (
                    terms[b * rows : (b + 1) * rows] + (re * c - im * s),
                    terms[half + b * rows : half + (b + 1) * rows] + (re * s + im * c),
                )
            scale = 1.0 / math.sqrt(POINTS)
            alive = start + iota((rows, chunk), 1) < live
            re = jnp.where(alive, observed_ref[slot, 0, :, at] - re * scale, 0.0)
            im = jnp.where(alive, observed_ref[slot, 1, :, at] - im * scale, 0.0)
            residual_ref[slot, 0, :, at] = re.astype(jnp.bfloat16)
            residual_ref[slot, 1, :, at] = im.astype(jnp.bfloat16)


def image_kernel(
    facets,
    slots,
    owner_ref,
    update_ref,
    back_ref,
    lift_ref,
    table_ref,
    image_ref,
    lhs,
    taken,
    place,
):
    me = lax.axis_index("facet")
    subgrids = owner_ref.shape[0]
    rows = update_ref.shape[1]
    width = image_ref.shape[2]

    def clear(index, _):
        taken[index] = 0
        return 0

    lax.fori_loop(0, facets, clear, 0, unroll=True)

    def assign(index, _):
        holder = owner_ref[index]
        rank = taken[holder]
        taken[holder] = rank + 1
        place[index] = position_of(holder, me, facets) * slots + rank
        return 0

    lax.fori_loop(0, subgrids, assign, 0, unroll=True)

    def lift(index, _):
        value = update_ref[place[index]].astype(jnp.float32)
        turned = jnp.concatenate([swap(block) for block in blocks_of(value)], 1)
        at = pl.ds(pl.multiple_of(index * SPLIT * rows, SPLIT * rows), SPLIT * rows)
        lhs[at, :] = jnp.concatenate(
            [
                value * lift_ref[0, part : part + 1, :] + turned * lift_ref[1, part : part + 1, :]
                for part in range(SPLIT)
            ],
            0,
        ).astype(jnp.bfloat16)
        return 0

    lax.fori_loop(0, subgrids, lift, 0, unroll=True)
    back = jnp.dot(lhs[...], table_ref[...], preferred_element_type=jnp.float32)
    wide = width // SPLIT
    for part in range(SPLIT):
        at = slice(part * wide, (part + 1) * wide)
        out_re = jnp.zeros((rows, wide), jnp.float32)
        out_im = jnp.zeros((rows, wide), jnp.float32)
        for index in range(subgrids):
            first = (index * SPLIT + part) * rows
            re = back[first : first + rows, :wide]
            im = back[first : first + rows, wide:]
            c = back_ref[0, index : index + 1, at]
            s = back_ref[1, index : index + 1, at]
            out_re = out_re + (re * c - im * s)
            out_im = out_im + (re * s + im * c)
        image_ref[0, :, at] = out_re
        image_ref[1, :, at] = out_im


def gather(value, staged, facets):
    far = min(FAR, facets)
    near = facets // far
    pieces = [staged[None]]
    for step in range(1, far):
        pairs = [(index, (index + step * near) % facets) for index in range(facets)]
        pieces.append(lax.ppermute(value, "facet", pairs)[None])
    together = jnp.concatenate(pieces, 0)
    distance = near // 2
    while distance:
        pairs = [(index, index ^ distance) for index in range(facets)]
        received = lax.ppermute(together, "facet", pairs)
        together = jnp.concatenate([together, received], 0)
        distance //= 2
    return together


VMEM = pl.BlockSpec(memory_space=pltpu.VMEM)
SMEM = pl.BlockSpec(memory_space=pltpu.SMEM)
HBM = pl.BlockSpec(memory_space=pltpu.HBM)


def in_hbm(value):
    return pltpu.with_memory_space_constraint(value, pltpu.HBM)


def call(kernel, inputs, outputs, scratch, limit=8, places=None):
    return pl.pallas_call(
        kernel,
        in_specs=inputs,
        out_specs=places or jax.tree.map(lambda _: VMEM, outputs),
        out_shape=outputs,
        scratch_shapes=scratch,
        compiler_params=pltpu.CompilerParams(vmem_limit_bytes=limit << 20),
    )


def body(facets, sky_strips, prolate, subgrid_offset, owner, observed, vis_uv, vis_count):
    _, rows, width = sky_strips.shape
    slots, _, _, total = observed.shape
    subgrids = owner.shape[0]
    modulus = width * facets
    shape = jax.ShapeDtypeStruct
    weight = prolate.reshape(1, width)
    mod, turns, live, staged, uv, visibilities = call(
        functools.partial(setup_kernel, modulus, slots),
        [HBM] * 7,
        (
            shape((2, slots, facets, width), jnp.float32),
            shape((2, facets * SPLIT, 2 * POINTS), jnp.float32),
            shape((slots, rows, 128), jnp.int32),
            shape(sky_strips.shape, sky_strips.dtype),
            shape(vis_uv.shape, vis_uv.dtype),
            shape(observed.shape, observed.dtype),
        ),
        [
            pltpu.SMEM((subgrids,), jnp.int32),
            pltpu.SMEM((subgrids,), jnp.int32),
            pltpu.SMEM((slots,), jnp.int32),
            pltpu.VMEM((1, width), jnp.float32),
            pltpu.SemaphoreType.DMA((7,)),
        ],
    )(*(in_hbm(value) for value in (owner, subgrid_offset, vis_count, weight, sky_strips, vis_uv, observed)))
    table = call(
        functools.partial(table_kernel, modulus),
        [],
        shape((2 * width // SPLIT, 2 * POINTS), jnp.bfloat16),
        [pltpu.VMEM((STEP, 2 * POINTS), jnp.float32)] * 2
        + [pltpu.VMEM((width // SPLIT // STEP, 2 * POINTS), jnp.float32)] * 2,
    )()
    back_table = call(
        functools.partial(back_table_kernel, modulus),
        [],
        shape((2 * POINTS, 2 * width // SPLIT), jnp.bfloat16),
        [pltpu.VMEM((BLOCK, width // SPLIT), jnp.float32)] * 2
        + [pltpu.VMEM((FINE, width // SPLIT), jnp.float32)] * 2,
    )()
    pieces = [
        call(
            functools.partial(observe_kernel, slot),
            [VMEM] * 3,
            (
                shape((BLOCK, total), jnp.bfloat16),
                shape((2, 8, total // 8), jnp.float32),
                shape((rows, 2 * POINTS), jnp.float32),
                shape((2, FINE, BLOCK), jnp.float32),
            ),
            [pltpu.VMEM((8, total // 8), jnp.float32)] * 7,
        )(uv, live, visibilities)
        for slot in range(slots)
    ]
    coarse, fine, seen, lags = zip(*pieces)
    matrices = call(
        functools.partial(toeplitz_kernel, slots),
        [VMEM] * slots,
        (shape((2 * BLOCK, 2 * FINE * BLOCK), jnp.bfloat16),) * slots,
        [],
    )(*lags)
    sky = gather(sky_strips, staged, facets)
    points, update = call(
        functools.partial(grid_kernel, facets, total),
        [VMEM] * (4 + 2 * slots),
        (
            shape((slots, 2 * FINE * rows, BLOCK), jnp.bfloat16),
            shape((slots, rows, 2 * POINTS), jnp.bfloat16),
        ),
        [
            pltpu.VMEM((slots * facets * SPLIT * rows, 2 * width // SPLIT), jnp.bfloat16),
            pltpu.VMEM((slots * facets * SPLIT * rows, 2 * POINTS), jnp.float32),
        ],
        16,
    )(sky, mod, turns, table, *seen, *matrices)
    residual = call(
        functools.partial(residual_kernel, slots),
        [VMEM] * (3 + 2 * slots),
        shape((slots, 2, rows, total), jnp.bfloat16),
        [],
        16,
    )(points, live, visibilities, *coarse, *fine)

    back, lift, residual = call(
        functools.partial(plan_kernel, modulus),
        [HBM] * 3 + [VMEM],
        (
            shape((2, subgrids, width), jnp.float32),
            shape((2, SPLIT, 2 * POINTS), jnp.float32),
            shape(residual.shape, residual.dtype),
        ),
        [
            pltpu.SMEM((subgrids,), jnp.int32),
            pltpu.SMEM((subgrids,), jnp.int32),
            pltpu.VMEM((1, width), jnp.float32),
            pltpu.SemaphoreType.DMA((4,)),
        ],
        places=(VMEM, VMEM, HBM),
    )(in_hbm(owner), in_hbm(subgrid_offset), in_hbm(weight), residual)
    updates = gather(update, update, facets).reshape(-1, rows, 2 * POINTS)
    image = call(
        functools.partial(image_kernel, facets, slots),
        [SMEM] + [VMEM] * 4,
        shape((2, rows, width), jnp.float32),
        [
            pltpu.VMEM((subgrids * SPLIT * rows, 2 * POINTS), jnp.bfloat16),
            pltpu.SMEM((facets,), jnp.int32),
            pltpu.SMEM((subgrids,), jnp.int32),
        ],
        16,
    )(owner, updates, back, lift, back_table)
    return residual, image


def local(facets, *arguments):
    return body(facets, *arguments)


def solution(mesh):
    in_specs = (
        P(None, "groups", "facet"),
        P(),
        P(),
        P(),
        P(("groups", "facet"), None, None, None),
        P(("groups", "facet"), None),
        P(("groups", "facet")),
    )
    out_specs = (P(("groups", "facet"), None, None, None), P(None, "groups", "facet"))
    return jax.shard_map(
        functools.partial(local, mesh.shape["facet"]),
        mesh=mesh,
        in_specs=in_specs,
        out_specs=out_specs,
        check_vma=False,
    )
```

time: 42.7 us -> 43.2 us (1.012)
  Pallas kernels: 15.2 us -> 15.8 us
    pallas_call x6 -> x7, Pallas kernels: 10.4 us -> 11.7 us  [the longest x2 4.52 us: body(): call(functools.partial(observe_kernel, slot), [VMEM] * 3, (shape((BLOCK,...]
    pallas_call x1, Pallas kernels: 1.7 us -> 0.93 us  [body(): call(functools.partial(back_table_kernel, modulus), [], shape((2 * POINTS...]
  transfers between devices with their start and end apart: 10 -> 10, of which waited for: 7 -> 6; matrix products, arithmetic and copies ran while one was open for 0% -> 0% of each run, Pallas kernels for 20% -> 27%
where the time goes in v3:
time: 43.2 us; the launch traced here: 43 us
  Pallas kernels  15.8 us (37%)
  starting transfers between devices  14.2 us (33%)
  waiting for transfers between devices  12 us (28%)
  between operations  0.8 us (2%)
    ppermute x6, starting transfers between devices, gather(): pieces.append(lax.ppermute(value, 'facet', pairs)[None])  10.9 us
    ppermute x4, waiting for transfers between devices, gather(): received = lax.ppermute(together, 'facet', pairs)  6.84 us
    ppermute x6, waiting for transfers between devices, gather(): pieces.append(lax.ppermute(value, 'facet', pairs)[None])  5.17 us
    pallas_call x2, Pallas kernels, body(): call(functools.partial(observe_kernel, slot), [VMEM] * 3, (shape((BLOCK,...  4.52 us
    ppermute x4, starting transfers between devices, gather(): received = lax.ppermute(together, 'facet', pairs)  3.31 us
    pallas_call x1, Pallas kernels, body(): call(functools.partial(image_kernel, facets, slots), [SMEM] + [VMEM] * 4,...  2.24 us
    pallas_call x1, Pallas kernels, body(): call(functools.partial(grid_kernel, facets, total), [VMEM] * (4 + 2 * slo...  1.96 us
    pallas_call x1, Pallas kernels, body(): call(functools.partial(residual_kernel, slots), [VMEM] * (3 + 2 * slots),...  1.71 us
  transfers between devices with their start and end apart: 10, of which 6 were waited for; matrix products, arithmetic and copies ran while one was open for 0% of the time, Pallas kernels for 27%

profile of v3, /device:TPU:0, one launch (start us, length us, event | category | flops | bytes accessed | tf_op | source)
XLA Modules:
  0.0 43.0 jit_solution(6967659607263221664)
XLA Ops:
  0.6 3.1 %collective-permute-start = (bf16[2,8,1024]{2,1,0:T(8,128)(2,1)}, bf16[2,8,1024]{2,1,0:T(8,128)(2,1)S(1)}, u32[]{:S(2)}, u32[]{:S(2)}) collective-permute-start(bf16[2,8,1024]{2,1,0:T(8,128)(2,1)} %sky_hbm.1), channel_id=1, source_target_pairs={{0,4},{1,5},{2,6},{3,7},{4,8},{5,9},{6,10},{7,11},{8,12},{9,13},{1... | collective-permute-start | bytes 98312 | tf_op jit(solution)/shard_map/ppermute | solution.py:539
  3.7 2.6 %collective-permute-start.1 = (bf16[2,8,1024]{2,1,0:T(8,128)(2,1)}, bf16[2,8,1024]{2,1,0:T(8,128)(2,1)S(1)}, u32[]{:S(2)}, u32[]{:S(2)}) collective-permute-start(bf16[2,8,1024]{2,1,0:T(8,128)(2,1)} %sky_hbm.1), channel_id=1, source_target_pairs={{0,8},{1,9},{2,10},{3,11},{4,12},{5,13},{6,14},{7,15},{8,0},{9,1},... | collective-permute-start | bytes 98312 | tf_op jit(solution)/shard_map/ppermute | solution.py:539
  6.3 1.3 %collective-permute-start.2 = (bf16[2,8,1024]{2,1,0:T(8,128)(2,1)}, bf16[2,8,1024]{2,1,0:T(8,128)(2,1)S(1)}, u32[]{:S(2)}, u32[]{:S(2)}) collective-permute-start(bf16[2,8,1024]{2,1,0:T(8,128)(2,1)} %sky_hbm.1), channel_id=1, source_target_pairs={{0,12},{1,13},{2,14},{3,15},{4,0},{5,1},{6,2},{7,3},{8,4},{9,5},{1... | collective-permute-start | bytes 98312 | tf_op jit(solution)/shard_map/ppermute | solution.py:539
  7.7 1.4 %shard_map.86 = (f32[2,2,16,1024]{3,2,1,0:T(8,128)S(1)}, f32[2,32,1024]{2,1,0:T(8,128)S(1)}, s32[2,8,128]{2,1,0:T(8,128)S(1)}, bf16[2,8,1024]{2,1,0:T(8,128)(2,1...) custom-call(s32[16]{0:T(128)} %owner_ref.1, s32[16]{0:T(128)} %offset_hbm.3, s32[2]{0:T(128)} %count_hbm.1, ...), custom_call_target="tpu_custom_call" | custom-call | tf_op jit(solution)/shard_map/pallas_call | solution.py:577
  9.1 0.0 collective-permute-done
  9.1 0.0 collective-permute-done.1
  9.1 1.3 %collective-permute-done.2 = bf16[2,8,1024]{2,1,0:T(8,128)(2,1)S(1)} collective-permute-done((bf16[2,8,1024]{2,1,0:T(8,128)(2,1)}, bf16[2,8,1024]{2,1,0:T(8,128)(2,1)S(1)}, u32[]{:S(2)}, u32[]{:S(2)}) %collective-permute-start.2) | collective-permute-done | bytes 32800 | tf_op jit(solution)/shard_map/ppermute | solution.py:539
  10.5 1.6 %collective-permute-start.3 = (bf16[4,2,8,1024]{3,2,1,0:T(8,128)(2,1)S(1)}, bf16[4,2,8,1024]{3,2,1,0:T(8,128)(2,1)S(1)}, u32[]{:S(2)}, u32[]{:S(2)}) collective-permute-start(bf16[4,2,8,1024]{3,2,1,0:T(8,128)(2,1)S(1)} %pad_maximum_fusion), channel_id=1, source_target_pairs={{0,2},{1,3},{2,0},{3,1},{4,6},{5,7},{6,4},{7,5},{8,10},{9,11},{10,... | collective-permute-start | bytes 393224 | tf_op jit(solution)/shard_map/ppermute | solution.py:544
  12.1 3.4 %collective-permute-done.3 = bf16[4,2,8,1024]{3,2,1,0:T(8,128)(2,1)S(1)} collective-permute-done((bf16[4,2,8,1024]{3,2,1,0:T(8,128)(2,1)S(1)}, bf16[4,2,8,1024]{3,2,1,0:T(8,128)(2,1)S(1)}, u32[]{:S(2)}, u32[]{:S(2)}) %collective-permute-start.3) | collective-permute-done | bytes 131104 | tf_op jit(solution)/shard_map/ppermute | solution.py:544
  15.5 0.1 collective-permute-start.4
  15.6 2.2 %shard_map.88 = (bf16[128,8192]{1,0:T(8,128)(2,1)S(1)}, f32[2,8,1024]{2,1,0:T(8,128)S(1)}, f32[8,1024]{1,0:T(8,128)S(1)}, f32[2,8,128]{2,1,0:T(8,128)S(1)}) custom-call(f32[2,8192]{1,0:T(2,128)S(1)} %get-tuple-element.26.uv_ref, s32[2,8,128]{2,1,0:T(8,128)S(1)} %get-tuple-element.27.live_ref, f32[2,2,8,8192]{3,2,1,0:T(8,128)S(1)} %get-tuple-element.28.observed_ref), custom_call_target="tpu_custom_call" | custom-call | tf_op jit(solution)/shard_map/pallas_call | solution.py:611
  17.8 2.3 %shard_map.89 = (bf16[128,8192]{1,0:T(8,128)(2,1)S(1)}, f32[2,8,1024]{2,1,0:T(8,128)S(1)}, f32[8,1024]{1,0:T(8,128)S(1)}, f32[2,8,128]{2,1,0:T(8,128)S(1)}) custom-call(f32[2,8192]{1,0:T(2,128)S(1)} %get-tuple-element.26.uv_ref, s32[2,8,128]{2,1,0:T(8,128)S(1)} %get-tuple-element.27.live_ref, f32[2,2,8,8192]{3,2,1,0:T(8,128)S(1)} %get-tuple-element.28.observed_ref), custom_call_target="tpu_custom_call" | custom-call | tf_op jit(solution)/shard_map/pallas_call | solution.py:611
  20.1 1.1 %shard_map.87.table_ref = bf16[1024,1024]{1,0:T(8,128)(2,1)S(1)} custom-call(), custom_call_target="tpu_custom_call" | custom-call | tf_op jit(solution)/shard_map/pallas_call | solution.py:596
  21.2 1.1 %shard_map.90 = (bf16[256,2048]{1,0:T(8,128)(2,1)S(1)}, bf16[256,2048]{1,0:T(8,128)(2,1)S(1)}) custom-call(f32[2,8,128]{2,1,0:T(8,128)S(1)} %get-tuple-element.31.refs_0_, f32[2,8,128]{2,1,0:T(8,128)S(1)} %get-tuple-element.32.refs_1_), custom_call_target="tpu_custom_call" | custom-call | tf_op jit(solution)/shard_map/pallas_call | solution.py:625
  22.3 0.0 collective-permute-done.4
  22.3 2.0 %shard_map.91 = (bf16[2,128,128]{2,1,0:T(8,128)(2,1)S(1)}, bf16[2,8,1024]{2,1,0:T(8,128)(2,1)S(1)}) custom-call(bf16[16,2,8,1024]{3,2,1,0:T(8,128)(2,1)S(1)} %constant_dynamic-update-slice_fusion.5.sky_ref, f32[2,2,16,1024]{3,2,1,0:T(8,128)S(1)} %get-tuple-element.24.mod_ref, f32[2,32,1024]{2,1,0:T(8,128)S(1)} %get-tuple-element.25.turn_ref, ...), custom_call_target="tpu_custom_call" | custom-call | tf_op jit(solution)/shard_map/pallas_call | solution.py:632
  24.3 0.3 collective-permute-start.5
  24.6 3.5 %collective-permute-start.6 = (bf16[2,8,1024]{2,1,0:T(8,128)(2,1)S(1)}, bf16[2,8,1024]{2,1,0:T(8,128)(2,1)S(1)}, u32[]{:S(2)}, u32[]{:S(2)}) collective-permute-start(bf16[2,8,1024]{2,1,0:T(8,128)(2,1)S(1)} %get-tuple-element.41), channel_id=1, source_target_pairs={{0,8},{1,9},{2,10},{3,11},{4,12},{5,13},{6,14},{7,15},{8,0},{9,1},... | collective-permute-start | bytes 98312 | tf_op jit(solution)/shard_map/ppermute | solution.py:539
  28.1 0.1 collective-permute-start.7
  28.2 2.2 %collective-permute-done.5 = bf16[2,8,1024]{2,1,0:T(8,128)(2,1)S(1)} collective-permute-done((bf16[2,8,1024]{2,1,0:T(8,128)(2,1)S(1)}, bf16[2,8,1024]{2,1,0:T(8,128)(2,1)S(1)}, u32[]{:S(2)}, u32[]{:S(2)}) %collective-permute-start.5) | collective-permute-done | bytes 32800 | tf_op jit(solution)/shard_map/ppermute | solution.py:539
  30.4 1.0 %collective-permute-done.6 = bf16[2,8,1024]{2,1,0:T(8,128)(2,1)S(1)} collective-permute-done((bf16[2,8,1024]{2,1,0:T(8,128)(2,1)S(1)}, bf16[2,8,1024]{2,1,0:T(8,128)(2,1)S(1)}, u32[]{:S(2)}, u32[]{:S(2)}) %collective-permute-start.6) | collective-permute-done | bytes 32800 | tf_op jit(solution)/shard_map/ppermute | solution.py:539
  31.4 0.5 %collective-permute-done.7 = bf16[2,8,1024]{2,1,0:T(8,128)(2,1)S(1)} collective-permute-done((bf16[2,8,1024]{2,1,0:T(8,128)(2,1)S(1)}, bf16[2,8,1024]{2,1,0:T(8,128)(2,1)S(1)}, u32[]{:S(2)}, u32[]{:S(2)}) %collective-permute-start.7) | collective-permute-done | bytes 32800 | tf_op jit(solution)/shard_map/ppermute | solution.py:539
  32.0 1.6 %collective-permute-start.8 = (bf16[4,2,8,1024]{3,2,1,0:T(8,128)(2,1)S(1)}, bf16[4,2,8,1024]{3,2,1,0:T(8,128)(2,1)S(1)}, u32[]{:S(2)}, u32[]{:S(2)}) collective-permute-start(bf16[4,2,8,1024]{3,2,1,0:T(8,128)(2,1)S(1)} %pad_maximum_fusion.1), channel_id=1, source_target_pairs={{0,2},{1,3},{2,0},{3,1},{4,6},{5,7},{6,4},{7,5},{8,10},{9,11},{10,... | collective-permute-start | bytes 393224 | tf_op jit(solution)/shard_map/ppermute | solution.py:544
  33.6 3.4 %collective-permute-done.8 = bf16[4,2,8,1024]{3,2,1,0:T(8,128)(2,1)S(1)} collective-permute-done((bf16[4,2,8,1024]{3,2,1,0:T(8,128)(2,1)S(1)}, bf16[4,2,8,1024]{3,2,1,0:T(8,128)(2,1)S(1)}, u32[]{:S(2)}, u32[]{:S(2)}) %collective-permute-start.8) | collective-permute-done | bytes 131104 | tf_op jit(solution)/shard_map/ppermute | solution.py:544
  37.1 0.1 collective-permute-start.9
  37.2 0.9 %shard_map.94.table_ref = bf16[1024,1024]{1,0:T(8,128)(2,1)S(1)} custom-call(), custom_call_target="tpu_custom_call" | custom-call | tf_op jit(solution)/shard_map/pallas_call | solution.py:603
  38.1 0.0 copy-start
  38.1 1.7 %shard_map.92.residual_ref = bf16[2,2,8,8192]{3,2,1,0:T(8,128)(2,1)S(1)} custom-call(bf16[2,128,128]{2,1,0:T(8,128)(2,1)S(1)} %get-tuple-element.35.points_ref, s32[2,8,128]{2,1,0:T(8,128)S(1)} %get-tuple-element.27.live_ref, f32[2,2,8,8192]{3,2,1,0:T(8,128)S(1)} %get-tuple-element.28.observed_ref, bf16[128,8192]{1,0:T(8,128)(2,1)S(1)} %get-tuple-element.36.refs_0_, ...), custom_call_target="tpu_custom_call" | custom-call | tf_op jit(solution)/shard_map/pallas_call | solution.py:645
  39.8 0.9 %shard_map.93 = (f32[2,16,1024]{2,1,0:T(8,128)S(1)}, f32[2,2,1024]{2,1,0:T(2,128)S(1)}, bf16[2,2,8,8192]{3,2,1,0:T(8,128)(2,1)}) custom-call(s32[16]{0:T(128)} %owner_ref.1, s32[16]{0:T(128)} %offset_hbm.3, f32[1,1024]{1,0:T(1,128)} %bitcast.36, bf16[2,2,8,8192]{3,2,1,0:T(8,128)(2,1)S(1)} %shard_map.92.residual_ref), custom_call_target="tpu_custom_call" | custom-call | tf_op jit(solution)/shard_map/pallas_call | solution.py:653
  40.7 0.0 collective-permute-done.9
  40.7 0.0 copy-done
  40.7 2.2 %shard_map.95 = f32[2,8,1024]{2,1,0:T(8,128)} custom-call(s32[16]{0:T(128)S(1)} %copy-done, bf16[32,8,1024]{2,1,0:T(8,128)(2,1)S(1)} %bitcast.26, f32[2,16,1024]{2,1,0:T(8,128)S(1)} %get-tuple-element.42.back_ref, f32[2,2,1024]{2,1,0:T(2,128)S(1)} %get-tuple-element.43.lift_ref, bf16[1024,1024]{1,0:T(8,128)(2,1)S(1)} %shard_map.94.table_ref), custom_call_target="tpu_custom_call" | custom-call | tf_op jit(solution)/shard_map/pallas_call | solution.py:670
  (14 shorter events, 0.2 us)
Async XLA Ops:
  0.6 8.4 %collective-permute-start = (bf16[2,8,1024]{2,1,0:T(8,128)(2,1)}, bf16[2,8,1024]{2,1,0:T(8,128)(2,1)S(1)}, u32[]{:S(2)}, u32[]{:S(2)}) collective-permute-start(bf16[2,8,1024]{2,1,0:T(8,128)(2,1)} %sky_hbm.1), channel_id=1, source_target_pairs={{0,4},{1,5},{2,6},{3,7},{4,8},{5,9},{6,10},{7,11},{8,12},{9,13},{1... | collective-permute-start | bytes 98312 | tf_op jit(solution)/shard_map/ppermute | solution.py:539
  3.7 5.4 %collective-permute-start.1 = (bf16[2,8,1024]{2,1,0:T(8,128)(2,1)}, bf16[2,8,1024]{2,1,0:T(8,128)(2,1)S(1)}, u32[]{:S(2)}, u32[]{:S(2)}) collective-permute-start(bf16[2,8,1024]{2,1,0:T(8,128)(2,1)} %sky_hbm.1), channel_id=1, source_target_pairs={{0,8},{1,9},{2,10},{3,11},{4,12},{5,13},{6,14},{7,15},{8,0},{9,1},... | collective-permute-start | bytes 98312 | tf_op jit(solution)/shard_map/ppermute | solution.py:539
  6.3 4.1 %collective-permute-start.2 = (bf16[2,8,1024]{2,1,0:T(8,128)(2,1)}, bf16[2,8,1024]{2,1,0:T(8,128)(2,1)S(1)}, u32[]{:S(2)}, u32[]{:S(2)}) collective-permute-start(bf16[2,8,1024]{2,1,0:T(8,128)(2,1)} %sky_hbm.1), channel_id=1, source_target_pairs={{0,12},{1,13},{2,14},{3,15},{4,0},{5,1},{6,2},{7,3},{8,4},{9,5},{1... | collective-permute-start | bytes 98312 | tf_op jit(solution)/shard_map/ppermute | solution.py:539
  10.5 5.0 %collective-permute-start.3 = (bf16[4,2,8,1024]{3,2,1,0:T(8,128)(2,1)S(1)}, bf16[4,2,8,1024]{3,2,1,0:T(8,128)(2,1)S(1)}, u32[]{:S(2)}, u32[]{:S(2)}) collective-permute-start(bf16[4,2,8,1024]{3,2,1,0:T(8,128)(2,1)S(1)} %pad_maximum_fusion), channel_id=1, source_target_pairs={{0,2},{1,3},{2,0},{3,1},{4,6},{5,7},{6,4},{7,5},{8,10},{9,11},{10,... | collective-permute-start | bytes 393224 | tf_op jit(solution)/shard_map/ppermute | solution.py:544
  15.5 6.8 %collective-permute-start.4 = (bf16[8,2,8,1024]{3,2,1,0:T(8,128)(2,1)S(1)}, bf16[8,2,8,1024]{3,2,1,0:T(8,128)(2,1)S(1)}, u32[]{:S(2)}, u32[]{:S(2)}) collective-permute-start(bf16[8,2,8,1024]{3,2,1,0:T(8,128)(2,1)S(1)} %get-tuple-element.46), channel_id=1, source_target_pairs={{0,1},{1,0},{2,3},{3,2},{4,5},{5,4},{6,7},{7,6},{8,9},{9,8},{10,11... | collective-permute-start | bytes 786440 | tf_op jit(solution)/shard_map/ppermute | solution.py:544
  24.3 6.1 %collective-permute-start.5 = (bf16[2,8,1024]{2,1,0:T(8,128)(2,1)S(1)}, bf16[2,8,1024]{2,1,0:T(8,128)(2,1)S(1)}, u32[]{:S(2)}, u32[]{:S(2)}) collective-permute-start(bf16[2,8,1024]{2,1,0:T(8,128)(2,1)S(1)} %get-tuple-element.41), channel_id=1, source_target_pairs={{0,4},{1,5},{2,6},{3,7},{4,8},{5,9},{6,10},{7,11},{8,12},{9,13},{1... | collective-permute-start | bytes 98312 | tf_op jit(solution)/shard_map/ppermute | solution.py:539
  24.6 6.8 %collective-permute-start.6 = (bf16[2,8,1024]{2,1,0:T(8,128)(2,1)S(1)}, bf16[2,8,1024]{2,1,0:T(8,128)(2,1)S(1)}, u32[]{:S(2)}, u32[]{:S(2)}) collective-permute-start(bf16[2,8,1024]{2,1,0:T(8,128)(2,1)S(1)} %get-tuple-element.41), channel_id=1, source_target_pairs={{0,8},{1,9},{2,10},{3,11},{4,12},{5,13},{6,14},{7,15},{8,0},{9,1},... | collective-permute-start | bytes 98312 | tf_op jit(solution)/shard_map/ppermute | solution.py:539
  28.1 3.9 %collective-permute-start.7 = (bf16[2,8,1024]{2,1,0:T(8,128)(2,1)S(1)}, bf16[2,8,1024]{2,1,0:T(8,128)(2,1)S(1)}, u32[]{:S(2)}, u32[]{:S(2)}) collective-permute-start(bf16[2,8,1024]{2,1,0:T(8,128)(2,1)S(1)} %get-tuple-element.41), channel_id=1, source_target_pairs={{0,12},{1,13},{2,14},{3,15},{4,0},{5,1},{6,2},{7,3},{8,4},{9,5},{1... | collective-permute-start | bytes 98312 | tf_op jit(solution)/shard_map/ppermute | solution.py:539
  32.0 5.0 %collective-permute-start.8 = (bf16[4,2,8,1024]{3,2,1,0:T(8,128)(2,1)S(1)}, bf16[4,2,8,1024]{3,2,1,0:T(8,128)(2,1)S(1)}, u32[]{:S(2)}, u32[]{:S(2)}) collective-permute-start(bf16[4,2,8,1024]{3,2,1,0:T(8,128)(2,1)S(1)} %pad_maximum_fusion.1), channel_id=1, source_target_pairs={{0,2},{1,3},{2,0},{3,1},{4,6},{5,7},{6,4},{7,5},{8,10},{9,11},{10,... | collective-permute-start | bytes 393224 | tf_op jit(solution)/shard_map/ppermute | solution.py:544
  37.1 3.6 %collective-permute-start.9 = (bf16[8,2,8,1024]{3,2,1,0:T(8,128)(2,1)S(1)}, bf16[8,2,8,1024]{3,2,1,0:T(8,128)(2,1)S(1)}, u32[]{:S(2)}, u32[]{:S(2)}) collective-permute-start(bf16[8,2,8,1024]{3,2,1,0:T(8,128)(2,1)S(1)} %get-tuple-element.44), channel_id=1, source_target_pairs={{0,1},{1,0},{2,3},{3,2},{4,5},{5,4},{6,7},{7,6},{8,9},{9,8},{10,11... | collective-permute-start | bytes 786440 | tf_op jit(solution)/shard_map/ppermute | solution.py:544
  38.1 2.7 %copy-start = (s32[16]{0:T(128)S(1)}, s32[16]{0:T(128)}, u32[]{:S(2)}) copy-start(s32[16]{0:T(128)} %owner_ref.1) | copy-start | bytes 196
